TPU v7x, 32 devices: a whole 2x2x4 slice. The times are simulated.
32 devices in a mesh: section: 4 (over y, x), dp: 8 (over z, core).
Axes of the slice: x: 2, y: 2, z: 4, core: 2. Of those that a mesh axis runs over, the one named last changes fastest.
Arguments:
- activations: bfloat16 [4, 8, 257, 1792], P('section', 'dp'), may hold values from -6 to 6
- saved: bfloat16 [4, 8, 257, 1792], P('section', 'dp'), may hold values from -6 to 6
- cotangents: bfloat16 [4, 8, 257, 1792], P('section', 'dp'), may hold values from -1.1953125 to 1.1953125
- projection: bfloat16 [4, 1792, 1792], P('section'), may hold values from -0.125 to 0.125
- section_gain: float32 [4, 1792], P('section'), may hold values from 0.5 to 1.5
- final_gain: float32 [1792], replicated, may hold values from 0.5 to 1.5
- head_weight: bfloat16 [1792, 1024], P('section'), may hold values from -0.125 to 0.125
- text_embed: bfloat16 [8, 1024], P('dp'), may hold values from -6 to 6
- labels: int32 [8], P('dp'), may hold values from 0 to 7, each once
Outputs:
- next_act: bfloat16 [4, 8, 257, 1792], P('section', 'dp')
- next_grad: bfloat16 [4, 8, 257, 1792], P('section', 'dp')
- mean_loss: float32 [4], P('section')
Inputs may be any that keep to these rules, and one draw needn't show every extreme that they name: labels holds each caption index once.
All inputs are finite; a program needn't handle non-finite values.
Results may differ from a plain program's by a relative error of at most 0.0039.
Values may be sent and summed in bfloat16 or wider, within the bound.
No kernel may reach another device: no remote copies, remote signals or barrier semaphores. Data moves between devices by JAX's collectives and lax.ppermute only.
A program may use at most 64 MiB of HBM per device.

v0:
```python
import jax
import jax.numpy as jnp
from jax import lax
from jax.sharding import PartitionSpec as P

epsilon = 1e-06
logit_scale = 100.0


def shifted(value, axis, steps):
    count = lax.axis_size(axis)
    first, last = (max(0, -steps), min(count, count - steps))
    return lax.ppermute(value, axis, [(source, source + steps) for source in range(first, last)])


def spread(block, axis, owner):
    block = jnp.where(lax.axis_index(axis) == owner, block, jnp.zeros_like(block))
    return lax.psum(block, axis)


def norm_rows(values):
    centre = jnp.mean(values, axis=-1, keepdims=True)
    centred = values - centre
    variance = jnp.mean(centred * centred, axis=-1, keepdims=True)
    inverse = lax.rsqrt(variance + epsilon)
    return (centred * inverse, inverse)


def unit_rows(values):
    inverse = lax.rsqrt(jnp.sum(values * values, axis=-1, keepdims=True) + epsilon)
    return (values * inverse, inverse)


def forward_block(block_in, weight, scale_row):
    block_shape = block_in.shape
    standard, inverse = norm_rows(block_in.astype(jnp.float32))
    normed = (standard * scale_row).astype(jnp.bfloat16)
    mixed = jnp.dot(normed.reshape(-1, block_shape[-1]), weight, preferred_element_type=jnp.float32)
    return (block_in.astype(jnp.float32) + mixed.reshape(block_shape)).astype(jnp.bfloat16)


def backward_block(cotangent, restored, weight, scale_row):
    block_shape = restored.shape
    standard, inverse = norm_rows(restored.astype(jnp.float32))
    d_normed = lax.dot_general(
        cotangent.reshape(-1, block_shape[-1]),
        weight,
        (((1,), (1,)), ((), ())),
        preferred_element_type=jnp.float32,
    ).reshape(block_shape)
    d_standard = d_normed * scale_row
    d_input = cotangent.astype(jnp.float32) + inverse * (
        d_standard
        - jnp.mean(d_standard, axis=-1, keepdims=True)
        - standard * jnp.mean(d_standard * standard, axis=-1, keepdims=True)
    )
    return d_input.astype(jnp.bfloat16)


def contrastive(logits, label_values):
    count = logits.shape[0]
    targets = (label_values[:, None] == jnp.arange(count).astype(jnp.float32)[None, :]).astype(
        jnp.float32
    )
    row_lse = jax.nn.logsumexp(logits, axis=1)
    col_lse = jax.nn.logsumexp(logits, axis=0)
    picked = jnp.sum(logits * targets, axis=1)
    col_picked = jnp.sum(col_lse[None, :] * targets, axis=1)
    loss_value = 0.5 * jnp.mean(row_lse - picked) + 0.5 * jnp.mean(col_picked - picked)
    row_prob = jnp.exp(logits - row_lse[:, None])
    col_prob = jnp.exp(logits - col_lse[None, :])
    d_logits = 0.5 * (row_prob - targets + (col_prob - targets))
    return (loss_value, d_logits)


def local(
    activations,
    saved,
    cotangents,
    projection,
    section_gain,
    final_gain,
    head_weight,
    text_embed,
    labels,
):
    sections = lax.axis_size("section")
    section_index = lax.axis_index("section")
    is_last = section_index == sections - 1
    weight = projection[0]
    scale_row = section_gain[0]
    incoming = activations[0]
    block_out = forward_block(incoming, weight, scale_row)
    next_act = shifted(block_out[None], "section", 1)
    d_input = backward_block(cotangents[0], saved[0], weight, scale_row)
    passed_grad = shifted(d_input[None], "section", -1)
    pooled = jnp.mean(block_out.astype(jnp.float32), axis=1)
    pooled_std, pooled_inv = norm_rows(pooled)
    pooled_norm = (pooled_std * final_gain).astype(jnp.bfloat16)
    shared = spread(pooled_norm, "section", sections - 1)
    row_count = head_weight.shape[0]
    my_columns = lax.dynamic_slice_in_dim(shared, section_index * row_count, row_count, 1)
    embedding = lax.psum(
        jnp.dot(my_columns, head_weight, preferred_element_type=jnp.float32), "section"
    )
    image_unit, image_inv = unit_rows(embedding)
    own_count = image_unit.shape[0]
    text_unit, text_inv = unit_rows(text_embed.astype(jnp.float32))
    all_image, all_text, all_labels = (
        lax.all_gather(image_unit, "dp", axis=0, tiled=True),
        lax.all_gather(text_unit, "dp", axis=0, tiled=True),
        lax.all_gather(labels.astype(jnp.float32), "dp", axis=0, tiled=True),
    )
    logits = logit_scale * jnp.dot(all_image, all_text.T, precision=lax.Precision.HIGHEST)
    loss_value, d_logits = contrastive(logits, all_labels)
    own_rows = lax.dynamic_slice_in_dim(d_logits, lax.axis_index("dp") * own_count, own_count, 0)
    d_image = logit_scale * jnp.dot(own_rows, all_text, precision=lax.Precision.HIGHEST)
    d_embedding = (
        (d_image - image_unit * jnp.sum(d_image * image_unit, axis=-1, keepdims=True)) * image_inv
    ).astype(jnp.bfloat16)
    partial_value = lax.dot_general(
        d_embedding, head_weight, (((1,), (1,)), ((), ())), preferred_element_type=jnp.float32
    )
    d_pooled_norm = lax.all_gather(partial_value, "section", axis=1, tiled=True)
    d_std = d_pooled_norm * final_gain
    d_pooled = pooled_inv * (
        d_std
        - jnp.mean(d_std, axis=-1, keepdims=True)
        - pooled_std * jnp.mean(d_std * pooled_std, axis=-1, keepdims=True)
    )
    token_count = block_out.shape[1]
    loss_grad = jnp.broadcast_to((d_pooled / token_count)[:, None, :], block_out.shape).astype(
        jnp.bfloat16
    )
    next_grad = jnp.where(is_last, loss_grad[None], passed_grad)
    mean_loss = jnp.where(is_last, loss_value, jnp.float32(0.0))[None]
    return (next_act, next_grad, mean_loss)


def solution(mesh):
    return jax.shard_map(
        local,
        mesh=mesh,
        in_specs=(
            P("section", "dp", None, None),
            P("section", "dp", None, None),
            P("section", "dp", None, None),
            P("section", None, None),
            P("section", None),
            P(),
            P("section", None),
            P("dp", None),
            P("dp"),
        ),
        out_specs=(P("section", "dp", None, None), P("section", "dp", None, None), P("section")),
        check_vma=False,
    )
```

profile of v0, /device:TPU:0, one launch (start us, length us, event | category | flops | bytes accessed | tf_op | source)
XLA Modules:
  0.0 115.6 jit_solution(8883535703884968360)
XLA Ops:
  0.7 1.5 %convert_reduce_fusion = f32[257]{0:T(512)S(1)} fusion(bf16[1,1,257,1792]{3,2,1,0:T(8,128)(2,1)} %param.9), kind=kLoop, calls=%fused_computation.6 | loop fusion | flops 920831 | bytes 922116 | tf_op jit(solution)/shard_map/reduce_sum | solution.py:22
  2.2 1.6 %fusion.30 = f32[257]{0:T(512)S(1)} fusion(bf16[1,1,257,1792]{3,2,1,0:T(8,128)(2,1)} %param.9, f32[257]{0:T(512)S(1)} %broadcast_multiply_fusion.5), kind=kLoop, calls=%fused_computation.31 | loop fusion | flops 1841919 | bytes 923144 | tf_op jit(solution)/shard_map/reduce_sum | solution.py:24
  3.9 5.8 %convert_reduce_fusion.2 = (f32[1792]{0:T(1024)S(1)}, bf16[257,1792]{1,0:T(8,128)(2,1)}) fusion(bf16[1,1792,1792]{2,1,0:T(8,128)(2,1)} %param.12, bf16[1,1,257,1792]{3,2,1,0:T(8,128)(2,1)S(1)} %copy-done.2, f32[1792]{0:T(1024)S(1)} %reduce.23, f32[257]{0:T(512)S(1)} %add_rsqrt_fusion.1, f32[257]{0:T(512)S(1)} %broadcast_multiply_fusion.5), kind=kOutput, calls=%fused_computation.32 | convolution fusion | flops 1655193344 | bytes 8281096 | tf_op jit(solution)/shard_map/dot_general | solution.py:38
  9.7 5.0 %collective-permute-start = (bf16[1,1,257,1792]{3,2,1,0:T(8,128)(2,1)}, bf16[1,1,257,1792]{3,2,1,0:T(8,128)(2,1)S(1)}, u32[]{:S(2)}, u32[]{:S(2)}) collective-permute-start(bf16[1,1,257,1792]{3,2,1,0:T(8,128)(2,1)} %bitcast.4), channel_id=1, source_target_pairs={{0,8},{8,16},{16,24},{1,9},{9,17},{17,25},{2,10},{10,18},{18,26},{... | collective-permute-start | bytes 2763272 | tf_op jit(solution)/shard_map/ppermute | solution.py:13
  14.8 0.2 convert_reduce_fusion.1
  15.0 0.4 fusion.15
  15.4 4.9 %fusion.68 = (f32[257]{0:T(512)S(1)}, f32[257]{0:T(512)S(1)}, f32[257,1792]{1,0:T(8,128)S(1)}) fusion(f32[257]{0:T(512)S(1)} %add_rsqrt_fusion, f32[257]{0:T(512)S(1)} %broadcast_multiply_fusion.4, bf16[1,1,257,1792]{3,2,1,0:T(8,128)(2,1)S(1)} %copy-done.1, f32[1792]{0:T(1024)S(1)} %reduce.23, bf16[1,1792,1792]{2,1,0:T(8,128)(2,1)} %param.12, ...), kind=kOutput, calls=%fused_computation.102 | convolution fusion | flops 1653812992 | bytes 10118160 | tf_op jit(solution)/shard_map/dot_general | solution.py:45
  20.4 0.8 fusion.33
  21.2 1.3 %collective-permute-start.1 = (bf16[1,1,257,1792]{3,2,1,0:T(8,128)(2,1)S(1)}, bf16[1,1,257,1792]{3,2,1,0:T(8,128)(2,1)}, u32[]{:S(2)}, u32[]{:S(2)}) collective-permute-start(bf16[1,1,257,1792]{3,2,1,0:T(8,128)(2,1)S(1)} %fusion.33), channel_id=1, source_target_pairs={{8,0},{16,8},{24,16},{9,1},{17,9},{25,17},{10,2},{18,10},{26,18},{... | collective-permute-start | bytes 2763272 | tf_op jit(solution)/shard_map/ppermute | solution.py:13
  23.2 0.6 multiply_reduce_fusion.4
  24.5 0.6 dynamic-slice
  25.1 0.7 convert_dynamic-update-slice_fusion
  25.8 16.4 %all-reduce = f32[8]{0:T(128)S(1)} all-reduce(f32[8]{0:T(128)S(1)} %convert_dynamic-update-slice_fusion), channel_id=1, replica_groups=mesh['section'=4,'dp'=8] {'dp'}, use_global_device_ids=true, to_apply=%add | all-reduce | flops 8 | bytes 64
  42.2 14.1 %all-gather.2 = f32[8,1,1024]{2,1,0:T(1,128)S(1)} all-gather(f32[1,1,1024]{2,1,0:T(1,128)S(1)} %multiply_bitcast_fusion), channel_id=1, replica_groups=mesh['section'=4,'dp'=8] {'dp'}, dimensions={0}, use_global_device_ids=true | all-gather | bytes 36864 | tf_op jit(solution)/shard_map/all_gather | solution.py:111
  56.3 0.6 multiply_reduce_fusion.2
  57.5 0.6 multiply_reduce_fusion.1
  58.9 11.8 %psum.14 = bf16[1,1792]{1,0:T(2,128)(2,1)S(1)} all-reduce(bf16[1,1792]{1,0:T(2,128)(2,1)S(1)} %select_n.52), channel_id=1, replica_groups=mesh['section'=4,'dp'=8] {'section'}, use_global_device_ids=true, to_apply=%region_5.0 | all-reduce | flops 1792 | bytes 7168 | tf_op jit(solution)/shard_map/psum | solution.py:18
  70.7 0.3 fusion.58
  70.9 7.9 %psum.15 = f32[1,1024]{1,0:T(1,128)S(1)} all-reduce(f32[1,1024]{1,0:T(1,128)S(1)} %fusion.58), channel_id=1, replica_groups=mesh['section'=4,'dp'=8] {'section'}, use_global_device_ids=true, to_apply=%region_6.0 | all-reduce | flops 1024 | bytes 8192 | tf_op jit(solution)/shard_map/psum | solution.py:103
  78.8 0.6 multiply_reduce_fusion.5
  80.1 14.1 %all-gather.1 = f32[8,1,1024]{2,1,0:T(1,128)S(1)} all-gather(f32[1,1,1024]{2,1,0:T(1,128)S(1)} %fusion.67), channel_id=1, replica_groups=mesh['section'=4,'dp'=8] {'dp'}, dimensions={0}, use_global_device_ids=true | all-gather | bytes 36864 | tf_op jit(solution)/shard_map/all_gather | solution.py:110
  94.2 0.3 fusion.70
  94.5 0.2 fusion.49
  94.9 0.6 subtract_reduce_fusion
  95.8 0.6 dynamic-slice.1
  98.4 0.6 multiply_reduce_fusion.3
  99.0 1.0 fusion.52
  100.0 0.2 dynamic-update-slice.1
  100.2 9.2 %all-reduce.1 = f32[1792]{0:T(1024)S(1)} all-reduce(f32[1792]{0:T(1024)S(1)} %dynamic-update-slice.1), channel_id=2, replica_groups=mesh['section'=4,'dp'=8] {'section'}, use_global_device_ids=true, to_apply=%add.1 | all-reduce | flops 1792 | bytes 14336
  109.4 0.7 fusion.69
  111.4 2.2 %broadcast_select_fusion = bf16[1,1,257,1792]{3,2,1,0:T(8,128)(2,1)} fusion(bf16[1,1,257,1792]{3,2,1,0:T(8,128)(2,1)} %collective-permute-done.1, pred[]{:T(512)S(6)} %eq.8, bf16[1792]{0:T(1024)(128)(2,1)S(1)} %multiply_convert_fusion), kind=kLoop, calls=%fused_computation.40 | loop fusion | flops 460544 | bytes 1845761 | tf_op jit(solution)/shard_map/jit(_where)/select_n | solution.py:135
  113.6 0.9 copy.34
  (40 shorter events, 0.6 us)
Async XLA Ops:
  0.6 70.0 %copy-start = (bf16[448,1024]{1,0:T(8,128)(2,1)S(1)}, bf16[448,1024]{1,0:T(8,128)(2,1)}, u32[]{:S(2)}) copy-start(bf16[448,1024]{1,0:T(8,128)(2,1)} %param.15) | copy-start | bytes 2752516
  0.6 3.2 %copy-start.2 = (bf16[1,1,257,1792]{3,2,1,0:T(8,128)(2,1)S(1)}, bf16[1,1,257,1792]{3,2,1,0:T(8,128)(2,1)}, u32[]{:S(2)}) copy-start(bf16[1,1,257,1792]{3,2,1,0:T(8,128)(2,1)} %param.9) | copy-start | bytes 2763268
  0.7 3.2 %copy-start.6 = (f32[1,1792]{1,0:T(1,128)S(1)}, f32[1,1792]{1,0:T(1,128)}, u32[]{:S(2)}) copy-start(f32[1,1792]{1,0:T(1,128)} %param.13) | copy-start | bytes 21508
  3.9 10.9 %copy-start.1 = (bf16[1,1,257,1792]{3,2,1,0:T(8,128)(2,1)S(1)}, bf16[1,1,257,1792]{3,2,1,0:T(8,128)(2,1)}, u32[]{:S(2)}) copy-start(bf16[1,1,257,1792]{3,2,1,0:T(8,128)(2,1)} %param.10) | copy-start | bytes 2763268
  9.7 5.7 %copy-start.3 = (bf16[1,1,257,1792]{3,2,1,0:T(8,128)(2,1)S(1)}, bf16[1,1,257,1792]{3,2,1,0:T(8,128)(2,1)}, u32[]{:S(2)}) copy-start(bf16[1,1,257,1792]{3,2,1,0:T(8,128)(2,1)} %param.11) | copy-start | bytes 2763268
  9.7 101.7 %collective-permute-start = (bf16[1,1,257,1792]{3,2,1,0:T(8,128)(2,1)}, bf16[1,1,257,1792]{3,2,1,0:T(8,128)(2,1)S(1)}, u32[]{:S(2)}, u32[]{:S(2)}) collective-permute-start(bf16[1,1,257,1792]{3,2,1,0:T(8,128)(2,1)} %bitcast.4), channel_id=1, source_target_pairs={{0,8},{8,16},{16,24},{1,9},{9,17},{17,25},{2,10},{10,18},{18,26},{... | collective-permute-start | bytes 2763272 | tf_op jit(solution)/shard_map/ppermute | solution.py:13
  20.4 2.8 %copy-start.5 = (bf16[1,1024]{1,0:T(2,128)(2,1)S(1)}, bf16[1,1024]{1,0:T(2,128)(2,1)}, u32[]{:S(2)}) copy-start(bf16[1,1024]{1,0:T(2,128)(2,1)} %param.16) | copy-start | bytes 6148
  20.4 4.0 %copy-start.8 = (u32[32]{0:T(128)S(1)}, u32[32]{0:T(128)}, u32[]{:S(2)}) copy-start(u32[32]{0:T(128)} %constant.76) | copy-start | bytes 388
  20.4 38.4 %copy-start.4 = (f32[1792]{0:T(1024)S(1)}, f32[1792]{0:T(1024)}, u32[]{:S(2)}) copy-start(f32[1792]{0:T(1024)} %param.14) | copy-start | bytes 21508
  20.4 75.4 %copy-start.7 = (u32[32]{0:T(128)S(1)}, u32[32]{0:T(128)}, u32[]{:S(2)}) copy-start(u32[32]{0:T(128)} %constant.81) | copy-start | bytes 388
  21.2 90.2 %collective-permute-start.1 = (bf16[1,1,257,1792]{3,2,1,0:T(8,128)(2,1)S(1)}, bf16[1,1,257,1792]{3,2,1,0:T(8,128)(2,1)}, u32[]{:S(2)}, u32[]{:S(2)}) collective-permute-start(bf16[1,1,257,1792]{3,2,1,0:T(8,128)(2,1)S(1)} %fusion.33), channel_id=1, source_target_pairs={{8,0},{16,8},{24,16},{9,1},{17,9},{25,17},{10,2},{18,10},{26,18},{... | collective-permute-start | bytes 2763272 | tf_op jit(solution)/shard_map/ppermute | solution.py:13
where the time goes:
time: 116 us
  blocking collectives  73.4 us (63%)
  matrix products  12.5 us (11%)
  other arithmetic  12.4 us (11%)
  between operations  8.64 us (7%)
  starting transfers between devices  6.34 us (5%)
  local copies, waits for them, and re-layouts  2.44 us (2%)
    unnamed x2, blocking collectives  25.5 us
    all_gather x1, blocking collectives, local(): lax.all_gather(image_unit, 'dp', axis=0, tiled=True)  14.1 us
    all_gather x1, blocking collectives, local(): lax.all_gather(text_unit, 'dp', axis=0, tiled=True)  14.1 us
    psum x1, blocking collectives, spread(): return lax.psum(block, axis)  11.8 us
    psum x1, blocking collectives, local(): lax.psum(jnp.dot(my_columns, head_weight, preferred_element_type=jnp.floa...  7.87 us
    ppermute x2, starting transfers between devices, shifted(): lax.ppermute(value, axis, [(source, source + steps) for source in range(f...  6.34 us
    dot_general x1, matrix products, forward_block(): jnp.dot(normed.reshape(-1, block_shape[-1]), weight, preferred_element_ty...  5.82 us
    dot_general x1, matrix products, backward_block(): lax.dot_general(cotangent.reshape(-1, block_shape[-1]), weight, (((1,), (...  4.94 us
  transfers between devices with their start and end apart: 2, of which 0 were waited for; matrix products, arithmetic and copies ran while one was open for 13% of the time, Pallas kernels for 0%

commit v1 on v0

--- a/solution.py
+++ b/solution.py
@@ -1,10 +1,452 @@
+import functools
+
 import jax
 import jax.numpy as jnp
 from jax import lax
+from jax.experimental import pallas as pl
+from jax.experimental.pallas import tpu as pltpu
 from jax.sharding import PartitionSpec as P
+
 
 epsilon = 1e-06
 logit_scale = 100.0
+lane = 128
+F32 = jnp.float32
+BF16 = jnp.bfloat16
+
+
+def shift_pairs(count, steps):
+    first, last = (max(0, -steps), min(count, count - steps))
+    return [(source, source + steps) for source in range(first, last)]
+
+
+def vmem(count):
+    return [pl.BlockSpec(memory_space=pltpu.VMEM)] * count
+
+
+def row_stats(values):
+    width = values.shape[-1]
+    centre = jnp.sum(values, axis=-1, keepdims=True) * (1.0 / width)
+    centred = values - centre
+    variance = jnp.sum(centred * centred, axis=-1, keepdims=True) * (1.0 / width)
+    return centre, centred, lax.rsqrt(variance + epsilon)
+
+
+def thirds(values):
+    high = values.astype(BF16).astype(F32)
+    rest = values - high
+    middle = rest.astype(BF16).astype(F32)
+    low = (rest - middle).astype(BF16).astype(F32)
+    return high, middle, low
+
+
+NN = (((1,), (0,)), ((), ()))
+NT = (((1,), (1,)), ((), ()))
+
+
+def dot(left, right, form):
+    return lax.dot_general(left, right, form, preferred_element_type=F32)
+
+
+def tiles_of(depth):
+    width = 256 if depth % 256 == 0 else lane
+    return [(start, start + width) for start in range(0, depth, width)]
+
+
+def put(outs, low, high, block):
+    start = 0
+    for out in outs:
+        out[:, low:high] = block[start : start + out.shape[0]]
+        start += out.shape[0]
+
+
+def forward_kernel(act, gain, weight, pooled, *outs):
+    values = act[...].astype(F32)
+    _, centred, inverse = row_stats(values)
+    normed = (centred * inverse * gain[...]).astype(BF16)
+    for low, high in tiles_of(act.shape[1]):
+        mixed = dot(normed, weight[:, low:high], NN)
+        block = (act[:, low:high].astype(F32) + mixed).astype(BF16)
+        put(outs, low, high, block)
+        pooled[:, low:high] = jnp.sum(block.astype(F32), axis=0, keepdims=True) * (
+            1.0 / act.shape[0]
+        )
+
+
+def limit(mib):
+    return pltpu.CompilerParams(vmem_limit_bytes=mib * 2**20)
+
+
+def block_cost(rows, depth):
+    return pl.CostEstimate(
+        flops=2 * rows * depth * depth, bytes_accessed=2 * depth * depth, transcendentals=0
+    )
+
+
+def forward_block(act, gain, weight, cuts):
+    rows, depth = act.shape
+    parts = [jax.ShapeDtypeStruct((count, depth), BF16) for count in cuts]
+    return pl.pallas_call(
+        forward_kernel,
+        in_specs=vmem(3),
+        out_specs=vmem(1 + len(cuts)),
+        out_shape=[jax.ShapeDtypeStruct((1, depth), F32)] + parts,
+        compiler_params=limit(20),
+        cost_estimate=block_cost(rows, depth),
+        name="forward_block",
+    )(act, gain, weight)
+
+
+def backward_kernel(cot, saved, gain, weight, *refs):
+    outs, grads = refs[:-1], refs[-1]
+    depth = cot.shape[1]
+    centre, _, inverse = row_stats(saved[...].astype(F32))
+    total, total_unit = 0.0, 0.0
+    for low, high in tiles_of(depth):
+        grad = dot(cot[...], weight[low:high], NT) * gain[:, low:high]
+        grads[:, low:high] = grad
+        total = total + jnp.sum(grad, axis=-1, keepdims=True)
+        unit = (saved[:, low:high].astype(F32) - centre) * inverse
+        total_unit = total_unit + jnp.sum(grad * unit, axis=-1, keepdims=True)
+    mean = total * (1.0 / depth)
+    mean_unit = total_unit * (1.0 / depth)
+    for low, high in tiles_of(depth):
+        unit = (saved[:, low:high].astype(F32) - centre) * inverse
+        block = inverse * (grads[:, low:high] - mean - unit * mean_unit)
+        put(outs, low, high, (cot[:, low:high].astype(F32) + block).astype(BF16))
+
+
+def backward_block(cot, saved, gain, weight, cuts):
+    rows, depth = cot.shape
+    return pl.pallas_call(
+        backward_kernel,
+        in_specs=vmem(4),
+        out_specs=vmem(len(cuts)),
+        out_shape=[jax.ShapeDtypeStruct((count, depth), BF16) for count in cuts],
+        scratch_shapes=[pltpu.VMEM((rows, depth), F32)],
+        compiler_params=limit(20),
+        cost_estimate=block_cost(rows, depth),
+        name="backward_block",
+    )(cot, saved, gain, weight)
+
+
+def tail_rows(rows):
+    return -(-(rows + lane) // lane)
+
+
+def pack_kernel(rows, text, head, pack):
+    values = text[...].astype(F32)
+    unit = values * lax.rsqrt(jnp.sum(values * values, axis=-1, keepdims=True) + epsilon)
+    pieces = jnp.concatenate(thirds(unit) + (jnp.zeros((5, unit.shape[1]), F32),), axis=0)
+    shadow = jnp.sum(dot(pieces.astype(BF16), head[...], NT), axis=0, keepdims=True)
+    count = tail_rows(rows)
+    shadow = jnp.concatenate([shadow, jnp.zeros((1, count * lane - rows), F32)], axis=1)
+    start = lax.rem(lax.axis_index("section") * rows, lane)
+    shadow = pltpu.roll(jnp.broadcast_to(shadow, (8, count * lane)), start, 1)[0:1]
+    lines = [
+        part[:, lane * tile : lane * (tile + 1)] for part in thirds(shadow) for tile in range(count)
+    ]
+    height = pack.shape[0] - rows
+    lines.append(jnp.zeros((height - len(lines), lane), F32))
+    width = pack.shape[1]
+    mine = pl.ds(pl.multiple_of(lax.axis_index("dp") * width, width), width)
+    pack[:rows] = head[:, mine]
+    pack[rows:] = jnp.concatenate(lines, axis=0).astype(BF16)
+
+
+def pack_head(text, head, devices):
+    rows, width = head.shape
+    height = rows + -(-3 * tail_rows(rows) // 16) * 16
+    return pl.pallas_call(
+        functools.partial(pack_kernel, rows),
+        in_specs=vmem(2),
+        out_specs=pl.BlockSpec(memory_space=pltpu.VMEM),
+        out_shape=jax.ShapeDtypeStruct((height, width // devices), BF16),
+        compiler_params=limit(4),
+        cost_estimate=pl.CostEstimate(
+            flops=4 * 10**9, bytes_accessed=2 * rows * width, transcendentals=0
+        ),
+        name="pack_head",
+    )(text, head)
+
+
+def features_kernel(rows, pooled, gain, label, *refs):
+    packs, (message, standard) = refs[:-2], refs[-2:]
+    depth = pooled.shape[1]
+    count = tail_rows(rows)
+    tiles = [jnp.zeros((1, lane), F32)] * (depth // lane + count)
+    for section, pack in enumerate(packs):
+        tail = pack[rows:].astype(F32)
+        for tile in range(count):
+            place = section * rows // lane + tile
+            tiles[place] = tiles[place] + sum(
+                tail[part * count + tile : part * count + tile + 1] for part in range(3)
+            )
+    message[:, :depth] = jnp.concatenate(tiles[: depth // lane], axis=1)
+    _, centred, inverse = row_stats(pooled[...])
+    unit = centred * inverse
+    standard[:, :depth] = unit
+    standard[:, depth:] = jnp.broadcast_to(inverse, (1, lane))
+    message[:, depth : 2 * depth] = (unit * gain[...]).astype(BF16).astype(F32)
+    message[:, 2 * depth :] = jnp.full((1, lane), label[0], jnp.int32).astype(F32)
+
+
+def features(pooled, gain, label, packs, rows):
+    depth = pooled.shape[1]
+    return pl.pallas_call(
+        functools.partial(features_kernel, rows),
+        in_specs=vmem(2) + [pl.BlockSpec(memory_space=pltpu.SMEM)] + vmem(len(packs)),
+        out_specs=vmem(2),
+        out_shape=[
+            jax.ShapeDtypeStruct((1, 2 * depth + lane), F32),
+            jax.ShapeDtypeStruct((1, depth + lane), F32),
+        ],
+        compiler_params=limit(4),
+        name="features",
+    )(pooled, gain, label, *packs)
+
+
+def embed_kernel(rows, depth, table, *refs):
+    packs, (keep, send, scores, column) = refs[:-4], refs[-4:]
+    count = table.shape[0]
+    half = count // 2
+    for section, pack in enumerate(packs):
+        column[section * rows : (section + 1) * rows] = pack[:rows]
+    normed = table[:, depth : 2 * depth].astype(BF16)
+    weight = column[...]
+    embedding = dot(normed, weight, NN)
+    pieces = jnp.concatenate(thirds(embedding), axis=0).astype(BF16)
+    product = dot(pieces, weight, NT)
+    product = product[:count] + product[count : 2 * count] + product[2 * count :]
+    shadow = jnp.concatenate(thirds(table[:, :depth]), axis=0).astype(BF16)
+    score = dot(normed, shadow, NT)
+    score = score[:, :count] + score[:, count : 2 * count] + score[:, 2 * count :]
+    scores[...] = jnp.concatenate([score, jnp.zeros((count, lane - count), F32)], axis=1)
+    square = jnp.sum(embedding * embedding, axis=-1, keepdims=True)
+    place = lax.broadcasted_iota(jnp.int32, (count, lane), 0)
+    across = lax.broadcasted_iota(jnp.int32, (count, lane), 1)
+    square = jnp.sum(jnp.where(place == across, square, 0.0), axis=0, keepdims=True)
+    square = jnp.broadcast_to(square, (half, lane))
+    keep[:, :depth] = product[:half]
+    keep[:, depth:] = square
+    send[:, :depth] = product[half:]
+    send[:, depth:] = square
+
+
+def embed(table, packs, rows, depth):
+    count = table.shape[0]
+    part = jax.ShapeDtypeStruct((count // 2, depth + lane), F32)
+    return pl.pallas_call(
+        functools.partial(embed_kernel, rows, depth),
+        in_specs=vmem(1 + len(packs)),
+        out_specs=vmem(3),
+        out_shape=[part, part, jax.ShapeDtypeStruct((count, lane), F32)],
+        scratch_shapes=[pltpu.VMEM((depth, packs[0].shape[1]), BF16)],
+        compiler_params=limit(4),
+        name="embed",
+    )(table, *packs)
+
+
+def swapped(square, bit):
+    across = lax.broadcasted_iota(jnp.int32, square.shape, 1)
+    width = square.shape[1]
+    up = pltpu.roll(square, bit, 1)
+    down = pltpu.roll(square, width - bit, 1)
+    return jnp.where((across & bit) == 0, down, up)
+
+
+def fold_kernel(bit, depth, mine, theirs, keep, send):
+    half = mine.shape[0] // 2
+    total = mine[:, :depth] + theirs[:, :depth]
+    square = jnp.broadcast_to(mine[0:1, depth:], (8, lane)) + swapped(
+        jnp.broadcast_to(theirs[0:1, depth:], (8, lane)), bit
+    )
+    keep[:, :depth] = total[:half]
+    keep[:, depth:] = square[:half]
+    send[:, :depth] = total[half:]
+    send[:, depth:] = square[:half]
+
+
+def fold(mine, theirs, bit, depth):
+    part = jax.ShapeDtypeStruct((mine.shape[0] // 2, mine.shape[1]), F32)
+    return pl.pallas_call(
+        functools.partial(fold_kernel, bit, depth),
+        in_specs=vmem(2),
+        out_specs=vmem(2),
+        out_shape=[part, part],
+        compiler_params=limit(4),
+        name="fold",
+    )(mine, theirs)
+
+
+def loss_kernel(depth, tokens, mine, theirs, scores, table, standard, gain, grad, loss):
+    count = table.shape[0]
+    shape = (count, lane)
+    place = lax.broadcasted_iota(jnp.int32, shape, 0)
+    across = lax.broadcasted_iota(jnp.int32, shape, 1)
+    same = place == across
+    inside = across < count
+    square = jnp.broadcast_to(mine[0:1, depth:], (8, lane)) + swapped(
+        jnp.broadcast_to(theirs[0:1, depth:], (8, lane)), 1
+    )
+    square = jnp.broadcast_to(square[0:1], shape)
+    inverse = lax.rsqrt(jnp.sum(jnp.where(same, square, 0.0), axis=1, keepdims=True) + epsilon)
+    logits = logit_scale * inverse * scores[...]
+    owner = (across ^ lax.axis_index("dp")).astype(F32)
+    targets = jnp.where(inside & (table[:, 2 * depth : 2 * depth + 1] == owner), 1.0, 0.0)
+    masked = jnp.where(inside, logits, -jnp.inf)
+    row_max = jnp.max(masked, axis=1, keepdims=True)
+    row_lse = row_max + jnp.log(
+        jnp.sum(jnp.where(inside, jnp.exp(masked - row_max), 0.0), axis=1, keepdims=True)
+    )
+    col_max = jnp.max(logits, axis=0, keepdims=True)
+    col_lse = col_max + jnp.log(jnp.sum(jnp.exp(logits - col_max), axis=0, keepdims=True))
+    picked = jnp.sum(logits * targets, axis=1, keepdims=True)
+    col_picked = jnp.sum(col_lse * targets, axis=1, keepdims=True)
+    value = 0.5 / count * jnp.sum((row_lse - picked) + (col_picked - picked), axis=0, keepdims=True)
+    loss[...] = jnp.broadcast_to(value, loss.shape)
+    row_prob = jnp.where(inside, jnp.exp(masked - row_lse), 0.0)
+    col_prob = jnp.where(inside, jnp.exp(logits - col_lse), 0.0)
+    d_logits = (0.5 * (row_prob - targets + (col_prob - targets)))[0:1]
+    own_inverse = inverse[0:1]
+    along = jnp.sum(d_logits * logits[0:1], axis=1, keepdims=True)
+    weight = jnp.sum(
+        jnp.where(same, jnp.broadcast_to(d_logits, shape), 0.0), axis=1, keepdims=True
+    )
+    d_text = jnp.sum(weight * table[:, :depth], axis=0, keepdims=True)
+    product = mine[0:1, :depth] + theirs[0:1, :depth]
+    d_normed = own_inverse * (logit_scale * d_text - along * own_inverse * product)
+    d_unit = d_normed * gain[...]
+    unit = standard[:, :depth]
+    scale = 1.0 / depth
+    mean = jnp.sum(d_unit, axis=1, keepdims=True) * scale
+    mean_unit = jnp.sum(d_unit * unit, axis=1, keepdims=True) * scale
+    grad[...] = standard[:, depth : depth + 1] * (d_unit - mean - unit * mean_unit) * (1.0 / tokens)
+
+
+def loss_step(mine, theirs, scores, table, standard, gain, tokens):
+    depth = gain.shape[1]
+    return pl.pallas_call(
+        functools.partial(loss_kernel, depth, tokens),
+        in_specs=vmem(6),
+        out_specs=vmem(2),
+        out_shape=[
+            jax.ShapeDtypeStruct((1, depth), F32),
+            jax.ShapeDtypeStruct((1, lane), F32),
+        ],
+        compiler_params=limit(4),
+        name="loss_step",
+    )(mine, theirs, scores, table, standard, gain)
+
+
+def swap_dp(value, bit):
+    count = lax.axis_size("dp")
+    return lax.ppermute(value, "dp", [(index, index ^ bit) for index in range(count)])
+
+
+def finish_kernel(plan, *refs):
+    parts, (grad, loss, next_act, next_grad, mean_loss, wide, sems) = refs[:-7], refs[-7:]
+    sections = lax.axis_size("section")
+    mine = lax.axis_index("section")
+    mean_loss[...] = jnp.where(mine == sections - 1, loss[...], 0.0)
+    outs = (next_act, next_grad)
+    for section in range(sections):
+
+        @pl.when(mine == section)
+        def _(section=section):
+            copies = []
+            for target, start, sources in plan:
+                if target == 1 and section == sections - 1:
+                    continue
+                part = parts[sources[section]]
+                place = outs[target].at[pl.ds(start, part.shape[0])]
+                copies.append(pltpu.make_async_copy(part, place, sems.at[len(copies)]))
+            for copy in copies:
+                copy.start()
+            if section == sections - 1:
+                wide[...] = jnp.broadcast_to(grad[...], wide.shape).astype(BF16)
+                copies.append(pltpu.make_async_copy(wide, next_grad, sems.at[len(copies)]))
+                copies[-1].start()
+            for copy in copies:
+                copy.wait()
+
+
+def finish(plan, parts, grad, loss, tokens):
+    depth = grad.shape[1]
+    anywhere = pl.BlockSpec(memory_space=pl.ANY)
+    return pl.pallas_call(
+        functools.partial(finish_kernel, plan),
+        in_specs=vmem(len(parts) + 2),
+        out_specs=[anywhere, anywhere] + vmem(1),
+        out_shape=[jax.ShapeDtypeStruct((tokens, depth), BF16)] * 2
+        + [jax.ShapeDtypeStruct((1, lane), F32)],
+        scratch_shapes=[
+            pltpu.VMEM((tokens, depth), BF16),
+            pltpu.SemaphoreType.DMA((len(plan) + 1,)),
+        ],
+        compiler_params=limit(12),
+        name="finish",
+    )(*parts, grad, loss)
+
+
+def local(
+    activations,
+    saved,
+    cotangents,
+    projection,
+    section_gain,
+    final_gain,
+    head_weight,
+    text_embed,
+    labels,
+):
+    sections = lax.axis_size("section")
+    devices = lax.axis_size("dp")
+    section_index = lax.axis_index("section")
+    _, _, tokens, depth = activations.shape
+    rows = head_weight.shape[0]
+    act, kept, cot = (value.reshape(tokens, depth) for value in (activations, saved, cotangents))
+    relayed = sections == 4
+    first = tokens * 5 // 8 // 16 * 16
+    cuts = (first, tokens - first) if relayed else (tokens,)
+
+    pack = pack_head(text_embed, head_weight, devices)
+    packs = [
+        lax.ppermute(pack, "section", [(s, s ^ flip) for s in range(sections)])
+        for flip in range(sections - 1, 0, -1)
+    ] + [pack]
+    pooled, *acts = forward_block(act, section_gain, projection[0], cuts)
+    moved = [lax.ppermute(acts[0], "section", shift_pairs(sections, 1))]
+    grads = backward_block(cot, kept, section_gain, projection[0], cuts)
+    moved.append(lax.ppermute(grads[0], "section", shift_pairs(sections, -1)))
+    plan = [(0, 0, (0,) * sections), (1, 0, (1,) * sections)]
+    if relayed:
+        moved.append(lax.ppermute(acts[1], "section", [(0, 1), (2, 3)]))
+        moved.append(lax.ppermute(grads[1], "section", [(1, 0), (3, 2)]))
+        hand = jnp.where(section_index == 1, acts[1], grads[1])
+        hand = lax.ppermute(hand, "section", [(1, 3), (2, 0)])
+
+    gain = final_gain.reshape(1, depth)
+    message, standard = features(pooled, gain, labels, packs, rows)
+    table = message
+    bit = 1
+    while bit < devices:
+        other = swap_dp(table, bit)
+        table = jnp.concatenate([table, other], axis=0)
+        bit *= 2
+    mine, send, scores = embed(table, packs, rows, depth)
+    bit = devices // 2
+    while bit > 1:
+        other = swap_dp(send, bit)
+        mine, send = fold(mine, other, bit, depth)
+        bit //= 2
+    other = swap_dp(send, 1)
+    grad, loss = loss_step(mine, other, scores, table, standard, gain, tokens)
+    if relayed:
+        moved.append(lax.ppermute(hand, "section", [(3, 2), (0, 1)]))
+        plan += [(0, first, (2, 2, 4, 2)), (1, first, (3, 4, 3, 3))]
+    next_act, next_grad, mean_loss = finish(plan, moved, grad, loss, tokens)
+    return (next_act[None, None], next_grad[None, None], mean_loss[0, 0:1])
 
 
 def shifted(value, axis, steps):
@@ -31,15 +473,15 @@
     return (values * inverse, inverse)
 
 
-def forward_block(block_in, weight, scale_row):
+def plain_forward(block_in, weight, scale_row):
     block_shape = block_in.shape
-    standard, inverse = norm_rows(block_in.astype(jnp.float32))
+    standard, _ = norm_rows(block_in.astype(jnp.float32))
     normed = (standard * scale_row).astype(jnp.bfloat16)
     mixed = jnp.dot(normed.reshape(-1, block_shape[-1]), weight, preferred_element_type=jnp.float32)
     return (block_in.astype(jnp.float32) + mixed.reshape(block_shape)).astype(jnp.bfloat16)
 
 
-def backward_block(cotangent, restored, weight, scale_row):
+def plain_backward(cotangent, restored, weight, scale_row):
     block_shape = restored.shape
     standard, inverse = norm_rows(restored.astype(jnp.float32))
     d_normed = lax.dot_general(
@@ -73,7 +515,7 @@
     return (loss_value, d_logits)
 
 
-def local(
+def plain_local(
     activations,
     saved,
     cotangents,
@@ -90,9 +532,9 @@
     weight = projection[0]
     scale_row = section_gain[0]
     incoming = activations[0]
-    block_out = forward_block(incoming, weight, scale_row)
+    block_out = plain_forward(incoming, weight, scale_row)
     next_act = shifted(block_out[None], "section", 1)
-    d_input = backward_block(cotangents[0], saved[0], weight, scale_row)
+    d_input = plain_backward(cotangents[0], saved[0], weight, scale_row)
     passed_grad = shifted(d_input[None], "section", -1)
     pooled = jnp.mean(block_out.astype(jnp.float32), axis=1)
     pooled_std, pooled_inv = norm_rows(pooled)
@@ -105,7 +547,7 @@
     )
     image_unit, image_inv = unit_rows(embedding)
     own_count = image_unit.shape[0]
-    text_unit, text_inv = unit_rows(text_embed.astype(jnp.float32))
+    text_unit, _ = unit_rows(text_embed.astype(jnp.float32))
     all_image, all_text, all_labels = (
         lax.all_gather(image_unit, "dp", axis=0, tiled=True),
         lax.all_gather(text_unit, "dp", axis=0, tiled=True),
@@ -137,9 +579,21 @@
     return (next_act, next_grad, mean_loss)
 
 
+def fits(mesh, width):
+    sections, devices = mesh.shape["section"], mesh.shape["dp"]
+    powers = not (sections & (sections - 1)) and not (devices & (devices - 1))
+    return powers and sections > 1 and devices > 1 and width % (devices * lane) == 0
+
+
+def either(mesh, *args):
+    if fits(mesh, args[7].shape[1]):
+        return local(*args)
+    return plain_local(*args)
+
+
 def solution(mesh):
     return jax.shard_map(
-        local,
+        functools.partial(either, mesh),
         mesh=mesh,
         in_specs=(
             P("section", "dp", None, None),

time: 116 us -> 66.2 us (0.57)
  blocking collectives: 73.4 us -> 0 us
  waiting for transfers between devices: 0.01 us -> 26.3 us
  starting transfers between devices: 6.34 us -> 26 us
  matrix products: 12.5 us -> 0 us
  other arithmetic: 12.4 us -> 0.18 us
  Pallas kernels: 0 us -> 9.27 us
  between operations: 8.64 us -> 1.55 us
    all_gather x2 -> x0, blocking collectives: 28.2 us -> none  [the longest x1 14.1 us: local(): lax.all_gather(image_unit, 'dp', axis=0, tiled=True)]
    ppermute x2 -> x15, waiting for transfers between devices: 0.01 us -> 26.3 us  [the longest x6 9.32 us: swap_dp(): lax.ppermute(value, 'dp', [(index, index ^ bit) for index in range(count)])]
    unnamed x2 -> x0, blocking collectives: 25.5 us -> none
    psum x2 -> x0, blocking collectives: 19.7 us -> none  [the longest x1 11.8 us: spread(): return lax.psum(block, axis)]
    ppermute x2 -> x15, starting transfers between devices: 6.34 us -> 26 us  [the longest x1 6.63 us: local(): moved = [lax.ppermute(acts[0], 'section', shift_pairs(sections, 1))]]
    dot_general x6 -> x0, matrix products: 12.5 us -> none  [the longest x1 5.82 us: forward_block(): jnp.dot(normed.reshape(-1, block_shape[-1]), weight, preferred_element_ty...]
    pallas_call x0 -> x9, Pallas kernels: none -> 9.27 us  [the longest x1 3.03 us: backward_block(): pl.pallas_call(backward_kernel, in_specs=vmem(4), out_specs=vmem(len(cuts...]
    reduce_sum x13 -> x0, other arithmetic: 8.5 us -> none  [the longest x3 2.63 us: norm_rows(): variance = jnp.mean(centred * centred, axis=-1, keepdims=True)]
  transfers between devices with their start and end apart: 2 -> 15, of which waited for: 0 -> 6; matrix products, arithmetic and copies ran while one was open for 13% -> 0% of each run, Pallas kernels for 0% -> 10%
where the time goes in v1:
time: 66.2 us; the launch traced here: 65.9 us
  waiting for transfers between devices  26.3 us (40%)
  starting transfers between devices  26 us (39%)
  Pallas kernels  9.27 us (14%)
  local copies, waits for them, and re-layouts  2.63 us (4%)
  between operations  1.55 us (2%)
    ppermute x6, waiting for transfers between devices, swap_dp(): lax.ppermute(value, 'dp', [(index, index ^ bit) for index in range(count)])  9.32 us
    ppermute x1, waiting for transfers between devices, local(): moved.append(lax.ppermute(grads[1], 'section', [(1, 0), (3, 2)]))  7.6 us
    ppermute x1, waiting for transfers between devices, local(): moved.append(lax.ppermute(hand, 'section', [(3, 2), (0, 1)]))  6.75 us
    ppermute x1, starting transfers between devices, local(): moved = [lax.ppermute(acts[0], 'section', shift_pairs(sections, 1))]  6.63 us
    ppermute x6, starting transfers between devices, swap_dp(): lax.ppermute(value, 'dp', [(index, index ^ bit) for index in range(count)])  5 us
    ppermute x1, starting transfers between devices, local(): moved.append(lax.ppermute(acts[1], 'section', [(0, 1), (2, 3)]))  4.59 us
    ppermute x3, starting transfers between devices, local(): lax.ppermute(pack, 'section', [(s, s ^ flip) for s in range(sections)])  4.57 us
    pallas_call x1, Pallas kernels, backward_block(): pl.pallas_call(backward_kernel, in_specs=vmem(4), out_specs=vmem(len(cuts...  3.03 us
  transfers between devices with their start and end apart: 15, of which 6 were waited for; matrix products, arithmetic and copies ran while one was open for 0% of the time, Pallas kernels for 10%

profile of v1, /device:TPU:0, one launch (start us, length us, event | category | flops | bytes accessed | tf_op | source)
XLA Modules:
  0.0 65.9 jit_solution(17022752576735219306)
XLA Ops:
  0.7 1.3 %copy-done.5 = bf16[448,1024]{1,0:T(8,128)(2,1)S(1)} copy-done((bf16[448,1024]{1,0:T(8,128)(2,1)S(1)}, bf16[448,1024]{1,0:T(8,128)(2,1)}, u32[]{:S(2)}) %copy-start.5) | copy-done | bytes 917528
  2.0 1.3 %copy-done.6 = bf16[1,1024]{1,0:T(2,128)(2,1)S(1)} copy-done((bf16[1,1024]{1,0:T(2,128)(2,1)S(1)}, bf16[1,1024]{1,0:T(2,128)(2,1)}, u32[]{:S(2)}) %copy-start.6) | copy-done | bytes 2072
  3.3 0.5 pack_head.1.refs_3_
  3.8 3.0 %collective-permute-start.8 = (bf16[464,128]{1,0:T(8,128)(2,1)S(1)}, bf16[464,128]{1,0:T(8,128)(2,1)S(1)}, u32[]{:S(2)}, u32[]{:S(2)}) collective-permute-start(bf16[464,128]{1,0:T(8,128)(2,1)S(1)} %pack_head.1.refs_3_), channel_id=1, source_target_pairs={{0,8},{8,0},{16,24},{24,16},{1,9},{9,1},{17,25},{25,17},{2,10},{10... | collective-permute-start | bytes 356360 | tf_op jit(solution)/shard_map/ppermute | solution.py:415
  6.9 1.5 %collective-permute-start.7 = (bf16[464,128]{1,0:T(8,128)(2,1)S(1)}, bf16[464,128]{1,0:T(8,128)(2,1)S(1)}, u32[]{:S(2)}, u32[]{:S(2)}) collective-permute-start(bf16[464,128]{1,0:T(8,128)(2,1)S(1)} %pack_head.1.refs_3_), channel_id=1, source_target_pairs={{0,16},{8,24},{16,0},{24,8},{1,17},{9,25},{17,1},{25,9},{2,18},{10... | collective-permute-start | bytes 356360 | tf_op jit(solution)/shard_map/ppermute | solution.py:415
  8.4 0.0 collective-permute-start.6
  9.1 2.5 %forward_block.1 = (f32[1,1792]{1,0:T(1,128)S(1)}, bf16[160,1792]{1,0:T(8,128)(2,1)S(1)}, bf16[97,1792]{1,0:T(8,128)(2,1)S(1)}) custom-call(bf16[257,1792]{1,0:T(8,128)(2,1)S(1)} %bitcast.10, f32[1,1792]{1,0:T(1,128)S(1)} %copy-done.4, bf16[1792,1792]{1,0:T(8,128)(2,1)S(1)} %bitcast.8), custom_call_target="tpu_custom_call" | custom-call | flops 1650589696 | bytes 6422528 | tf_op jit(solution)/shard_map/forward_block/pallas_call | solution.py:89
  11.6 2.6 %collective-permute-done.7.refs_1_ = bf16[464,128]{1,0:T(8,128)(2,1)S(1)} collective-permute-done((bf16[464,128]{1,0:T(8,128)(2,1)S(1)}, bf16[464,128]{1,0:T(8,128)(2,1)S(1)}, u32[]{:S(2)}, u32[]{:S(2)}) %collective-permute-start.7) | collective-permute-done | bytes 118816 | tf_op jit(solution)/shard_map/ppermute | solution.py:415
  14.2 0.2 features.1
  14.4 0.1 collective-permute-start.9
  14.5 1.2 %collective-permute-done.9 = f32[1,3712]{1,0:T(1,128)S(1)} collective-permute-done((f32[1,3712]{1,0:T(1,128)S(1)}, f32[1,3712]{1,0:T(1,128)S(1)}, u32[]{:S(2)}, u32[]{:S(2)}) %collective-permute-start.9) | collective-permute-done | bytes 14880 | tf_op jit(solution)/shard_map/ppermute | solution.py:344
  15.7 1.6 %collective-permute-start.10 = (f32[2,3712]{1,0:T(2,128)S(1)}, f32[2,3712]{1,0:T(2,128)S(1)}, u32[]{:S(2)}, u32[]{:S(2)}) collective-permute-start(f32[2,3712]{1,0:T(2,128)S(1)} %pad_maximum_fusion.2), channel_id=1, source_target_pairs={{0,2},{1,3},{2,0},{3,1},{4,6},{5,7},{6,4},{7,5},{8,10},{9,11},{10,... | collective-permute-start | bytes 89096 | tf_op jit(solution)/shard_map/ppermute | solution.py:344
  17.4 3.0 %backward_block.1 = (bf16[160,1792]{1,0:T(8,128)(2,1)S(1)}, bf16[97,1792]{1,0:T(8,128)(2,1)S(1)}) custom-call(bf16[257,1792]{1,0:T(8,128)(2,1)S(1)} %bitcast.11, bf16[257,1792]{1,0:T(8,128)(2,1)S(1)} %bitcast.12, f32[1,1792]{1,0:T(1,128)S(1)} %copy-done.4, bf16[1792,1792]{1,0:T(8,128)(2,1)S(1)} %bitcast.9), custom_call_target="tpu_custom_call" | custom-call | flops 1650589696 | bytes 6422528 | tf_op jit(solution)/shard_map/backward_block/pallas_call | solution.py:121
  20.4 1.3 %collective-permute-start.1 = (bf16[160,1792]{1,0:T(8,128)(2,1)S(1)}, bf16[160,1792]{1,0:T(8,128)(2,1)S(1)}, u32[]{:S(2)}, u32[]{:S(2)}) collective-permute-start(bf16[160,1792]{1,0:T(8,128)(2,1)S(1)} %get-tuple-element.23), channel_id=1, source_target_pairs={{8,0},{16,8},{24,16},{9,1},{17,9},{25,17},{10,2},{18,10},{26,18},{... | collective-permute-start | bytes 1720328 | tf_op jit(solution)/shard_map/ppermute | solution.py:421
  21.8 2.6 %collective-permute-start.11 = (f32[4,3712]{1,0:T(4,128)S(1)}, f32[4,3712]{1,0:T(4,128)S(1)}, u32[]{:S(2)}, u32[]{:S(2)}) collective-permute-start(f32[4,3712]{1,0:T(4,128)S(1)} %pad_maximum_fusion.1), channel_id=1, source_target_pairs={{0,4},{1,5},{2,6},{3,7},{4,0},{5,1},{6,2},{7,3},{8,12},{9,13},{10,... | collective-permute-start | bytes 178184 | tf_op jit(solution)/shard_map/ppermute | solution.py:344
  24.5 1.3 %collective-permute-start.4 = (bf16[97,1792]{1,0:T(8,128)(2,1)S(1)}, bf16[97,1792]{1,0:T(8,128)(2,1)S(1)}, u32[]{:S(2)}, u32[]{:S(2)}) collective-permute-start(bf16[97,1792]{1,0:T(8,128)(2,1)S(1)} %broadcast_select_fusion), channel_id=1, source_target_pairs={{8,24},{16,0},{9,25},{17,1},{10,26},{18,2},{11,27},{19,3},{12,28},... | collective-permute-start | bytes 1042952 | tf_op jit(solution)/shard_map/ppermute | solution.py:427
  25.8 6.6 %collective-permute-start = (bf16[160,1792]{1,0:T(8,128)(2,1)S(1)}, bf16[160,1792]{1,0:T(8,128)(2,1)S(1)}, u32[]{:S(2)}, u32[]{:S(2)}) collective-permute-start(bf16[160,1792]{1,0:T(8,128)(2,1)S(1)} %get-tuple-element.22), channel_id=1, source_target_pairs={{0,8},{8,16},{16,24},{1,9},{9,17},{17,25},{2,10},{10,18},{18,26},{... | collective-permute-start | bytes 1720328 | tf_op jit(solution)/shard_map/ppermute | solution.py:419
  32.4 0.1 pad_maximum_fusion.table
  32.5 0.5 embed.1
  33.0 0.4 collective-permute-start.12
  33.4 4.7 %collective-permute-done.12.theirs = f32[4,1920]{1,0:T(4,128)S(1)} collective-permute-done((f32[4,1920]{1,0:T(4,128)S(1)}, f32[4,1920]{1,0:T(4,128)S(1)}, u32[]{:S(2)}, u32[]{:S(2)}) %collective-permute-start.12) | collective-permute-done | bytes 30752 | tf_op jit(solution)/shard_map/ppermute | solution.py:344
  38.1 0.1 fold.2
  38.1 0.3 collective-permute-start.13
  38.4 3.5 %collective-permute-done.13.theirs = f32[2,1920]{1,0:T(2,128)S(1)} collective-permute-done((f32[2,1920]{1,0:T(2,128)S(1)}, f32[2,1920]{1,0:T(2,128)S(1)}, u32[]{:S(2)}, u32[]{:S(2)}) %collective-permute-start.13) | collective-permute-done | bytes 15392 | tf_op jit(solution)/shard_map/ppermute | solution.py:344
  41.9 0.1 fold.3
  42.0 1.3 %collective-permute-start.3 = (bf16[97,1792]{1,0:T(8,128)(2,1)S(1)}, bf16[97,1792]{1,0:T(8,128)(2,1)S(1)}, u32[]{:S(2)}, u32[]{:S(2)}) collective-permute-start(bf16[97,1792]{1,0:T(8,128)(2,1)S(1)} %get-tuple-element.25), channel_id=1, source_target_pairs={{8,0},{24,16},{9,1},{25,17},{10,2},{26,18},{11,3},{27,19},{12,4},{... | collective-permute-start | bytes 1042952 | tf_op jit(solution)/shard_map/ppermute | solution.py:425
  43.3 4.6 %collective-permute-start.2 = (bf16[97,1792]{1,0:T(8,128)(2,1)S(1)}, bf16[97,1792]{1,0:T(8,128)(2,1)S(1)}, u32[]{:S(2)}, u32[]{:S(2)}) collective-permute-start(bf16[97,1792]{1,0:T(8,128)(2,1)S(1)} %get-tuple-element.24), channel_id=1, source_target_pairs={{0,8},{16,24},{1,9},{17,25},{2,10},{18,26},{3,11},{19,27},{4,12},{... | collective-permute-start | bytes 1042952 | tf_op jit(solution)/shard_map/ppermute | solution.py:424
  47.9 1.3 %collective-permute-start.5 = (bf16[97,1792]{1,0:T(8,128)(2,1)S(1)}, bf16[97,1792]{1,0:T(8,128)(2,1)S(1)}, u32[]{:S(2)}, u32[]{:S(2)}) collective-permute-start(bf16[97,1792]{1,0:T(8,128)(2,1)S(1)} %collective-permute-done.4), channel_id=1, source_target_pairs={{24,16},{0,8},{25,17},{1,9},{26,18},{2,10},{27,19},{3,11},{28,20},... | collective-permute-start | bytes 1042952 | tf_op jit(solution)/shard_map/ppermute | solution.py:446
  49.2 0.5 loss_step.1
  49.8 7.6 %collective-permute-done.3.refs_3_ = bf16[97,1792]{1,0:T(8,128)(2,1)S(1)} collective-permute-done((bf16[97,1792]{1,0:T(8,128)(2,1)S(1)}, bf16[97,1792]{1,0:T(8,128)(2,1)S(1)}, u32[]{:S(2)}, u32[]{:S(2)}) %collective-permute-start.3) | collective-permute-done | bytes 347680 | tf_op jit(solution)/shard_map/ppermute | solution.py:425
  57.4 6.8 %collective-permute-done.5.refs_4_ = bf16[97,1792]{1,0:T(8,128)(2,1)S(1)} collective-permute-done((bf16[97,1792]{1,0:T(8,128)(2,1)S(1)}, bf16[97,1792]{1,0:T(8,128)(2,1)S(1)}, u32[]{:S(2)}, u32[]{:S(2)}) %collective-permute-start.5) | collective-permute-done | bytes 347680 | tf_op jit(solution)/shard_map/ppermute | solution.py:446
  64.1 1.8 %finish.1 = (bf16[257,1792]{1,0:T(8,128)(2,1)}, bf16[257,1792]{1,0:T(8,128)(2,1)}, f32[1,128]{1,0:T(1,128)}) custom-call(bf16[160,1792]{1,0:T(8,128)(2,1)S(1)} %collective-permute-done.refs_0_, bf16[160,1792]{1,0:T(8,128)(2,1)S(1)} %collective-permute-done.1.refs_1_, bf16[97,1792]{1,0:T(8,128)(2,1)S(1)} %collective-permute-done.2.refs_2_, ...), custom_call_target="tpu_custom_call" | custom-call | tf_op jit(solution)/shard_map/finish/pallas_call | solution.py:377
  (28 shorter events, 0.2 us)
Async XLA Ops:
  0.6 8.4 %copy-start.4 = (f32[1,1792]{1,0:T(1,128)S(1)}, f32[1,1792]{1,0:T(1,128)}, u32[]{:S(2)}) copy-start(f32[1,1792]{1,0:T(1,128)} %gain.3) | copy-start | bytes 21508
  0.6 8.4 %copy-start = (bf16[1,1792,1792]{2,1,0:T(8,128)(2,1)S(1)}, bf16[1,1792,1792]{2,1,0:T(8,128)(2,1)}, u32[]{:S(2)}) copy-start(bf16[1,1792,1792]{2,1,0:T(8,128)(2,1)} %param.12) | copy-start | bytes 19267588
  0.7 8.4 %copy-start.1 = (bf16[1,1,257,1792]{3,2,1,0:T(8,128)(2,1)S(1)}, bf16[1,1,257,1792]{3,2,1,0:T(8,128)(2,1)}, u32[]{:S(2)}) copy-start(bf16[1,1,257,1792]{3,2,1,0:T(8,128)(2,1)} %param.9) | copy-start | bytes 2763268
  0.7 1.3 %copy-start.5 = (bf16[448,1024]{1,0:T(8,128)(2,1)S(1)}, bf16[448,1024]{1,0:T(8,128)(2,1)}, u32[]{:S(2)}) copy-start(bf16[448,1024]{1,0:T(8,128)(2,1)} %head.1) | copy-start | bytes 2752516
  2.0 1.3 %copy-start.6 = (bf16[1,1024]{1,0:T(2,128)(2,1)S(1)}, bf16[1,1024]{1,0:T(2,128)(2,1)}, u32[]{:S(2)}) copy-start(bf16[1,1024]{1,0:T(2,128)(2,1)} %text.1) | copy-start | bytes 6148
  3.3 5.8 %copy-start.7 = (f32[1792]{0:T(1024)S(1)}, f32[1792]{0:T(1024)}, u32[]{:S(2)}) copy-start(f32[1792]{0:T(1024)} %param.14) | copy-start | bytes 21508
  3.8 13.6 %copy-start.2 = (bf16[1,1,257,1792]{3,2,1,0:T(8,128)(2,1)S(1)}, bf16[1,1,257,1792]{3,2,1,0:T(8,128)(2,1)}, u32[]{:S(2)}) copy-start(bf16[1,1,257,1792]{3,2,1,0:T(8,128)(2,1)} %param.11) | copy-start | bytes 2763268
  3.8 13.6 %copy-start.3 = (bf16[1,1,257,1792]{3,2,1,0:T(8,128)(2,1)S(1)}, bf16[1,1,257,1792]{3,2,1,0:T(8,128)(2,1)}, u32[]{:S(2)}) copy-start(bf16[1,1,257,1792]{3,2,1,0:T(8,128)(2,1)} %param.10) | copy-start | bytes 2763268
  3.8 7.8 %collective-permute-start.8 = (bf16[464,128]{1,0:T(8,128)(2,1)S(1)}, bf16[464,128]{1,0:T(8,128)(2,1)S(1)}, u32[]{:S(2)}, u32[]{:S(2)}) collective-permute-start(bf16[464,128]{1,0:T(8,128)(2,1)S(1)} %pack_head.1.refs_3_), channel_id=1, source_target_pairs={{0,8},{8,0},{16,24},{24,16},{1,9},{9,1},{17,25},{25,17},{2,10},{10... | collective-permute-start | bytes 356360 | tf_op jit(solution)/shard_map/ppermute | solution.py:415
  6.9 7.4 %collective-permute-start.7 = (bf16[464,128]{1,0:T(8,128)(2,1)S(1)}, bf16[464,128]{1,0:T(8,128)(2,1)S(1)}, u32[]{:S(2)}, u32[]{:S(2)}) collective-permute-start(bf16[464,128]{1,0:T(8,128)(2,1)S(1)} %pack_head.1.refs_3_), channel_id=1, source_target_pairs={{0,16},{8,24},{16,0},{24,8},{1,17},{9,25},{17,1},{25,9},{2,18},{10... | collective-permute-start | bytes 356360 | tf_op jit(solution)/shard_map/ppermute | solution.py:415
  8.4 5.9 %collective-permute-start.6 = (bf16[464,128]{1,0:T(8,128)(2,1)S(1)}, bf16[464,128]{1,0:T(8,128)(2,1)S(1)}, u32[]{:S(2)}, u32[]{:S(2)}) collective-permute-start(bf16[464,128]{1,0:T(8,128)(2,1)S(1)} %pack_head.1.refs_3_), channel_id=1, source_target_pairs={{0,24},{8,16},{16,8},{24,0},{1,25},{9,17},{17,9},{25,1},{2,26},{10... | collective-permute-start | bytes 356360 | tf_op jit(solution)/shard_map/ppermute | solution.py:415
  14.4 1.2 %collective-permute-start.9 = (f32[1,3712]{1,0:T(1,128)S(1)}, f32[1,3712]{1,0:T(1,128)S(1)}, u32[]{:S(2)}, u32[]{:S(2)}) collective-permute-start(f32[1,3712]{1,0:T(1,128)S(1)} %get-tuple-element.27), channel_id=1, source_target_pairs={{0,1},{1,0},{2,3},{3,2},{4,5},{5,4},{6,7},{7,6},{8,9},{9,8},{10,11... | collective-permute-start | bytes 44552 | tf_op jit(solution)/shard_map/ppermute | solution.py:344
  15.7 6.0 %collective-permute-start.10 = (f32[2,3712]{1,0:T(2,128)S(1)}, f32[2,3712]{1,0:T(2,128)S(1)}, u32[]{:S(2)}, u32[]{:S(2)}) collective-permute-start(f32[2,3712]{1,0:T(2,128)S(1)} %pad_maximum_fusion.2), channel_id=1, source_target_pairs={{0,2},{1,3},{2,0},{3,1},{4,6},{5,7},{6,4},{7,5},{8,10},{9,11},{10,... | collective-permute-start | bytes 89096 | tf_op jit(solution)/shard_map/ppermute | solution.py:344
  20.4 36.9 %collective-permute-start.1 = (bf16[160,1792]{1,0:T(8,128)(2,1)S(1)}, bf16[160,1792]{1,0:T(8,128)(2,1)S(1)}, u32[]{:S(2)}, u32[]{:S(2)}) collective-permute-start(bf16[160,1792]{1,0:T(8,128)(2,1)S(1)} %get-tuple-element.23), channel_id=1, source_target_pairs={{8,0},{16,8},{24,16},{9,1},{17,9},{25,17},{10,2},{18,10},{26,18},{... | collective-permute-start | bytes 1720328 | tf_op jit(solution)/shard_map/ppermute | solution.py:421
  21.8 10.6 %collective-permute-start.11 = (f32[4,3712]{1,0:T(4,128)S(1)}, f32[4,3712]{1,0:T(4,128)S(1)}, u32[]{:S(2)}, u32[]{:S(2)}) collective-permute-start(f32[4,3712]{1,0:T(4,128)S(1)} %pad_maximum_fusion.1), channel_id=1, source_target_pairs={{0,4},{1,5},{2,6},{3,7},{4,0},{5,1},{6,2},{7,3},{8,12},{9,13},{10,... | collective-permute-start | bytes 178184 | tf_op jit(solution)/shard_map/ppermute | solution.py:344
  24.5 23.4 %collective-permute-start.4 = (bf16[97,1792]{1,0:T(8,128)(2,1)S(1)}, bf16[97,1792]{1,0:T(8,128)(2,1)S(1)}, u32[]{:S(2)}, u32[]{:S(2)}) collective-permute-start(bf16[97,1792]{1,0:T(8,128)(2,1)S(1)} %broadcast_select_fusion), channel_id=1, source_target_pairs={{8,24},{16,0},{9,25},{17,1},{10,26},{18,2},{11,27},{19,3},{12,28},... | collective-permute-start | bytes 1042952 | tf_op jit(solution)/shard_map/ppermute | solution.py:427
  25.8 31.6 %collective-permute-start = (bf16[160,1792]{1,0:T(8,128)(2,1)S(1)}, bf16[160,1792]{1,0:T(8,128)(2,1)S(1)}, u32[]{:S(2)}, u32[]{:S(2)}) collective-permute-start(bf16[160,1792]{1,0:T(8,128)(2,1)S(1)} %get-tuple-element.22), channel_id=1, source_target_pairs={{0,8},{8,16},{16,24},{1,9},{9,17},{17,25},{2,10},{10,18},{18,26},{... | collective-permute-start | bytes 1720328 | tf_op jit(solution)/shard_map/ppermute | solution.py:419
  33.0 5.0 %collective-permute-start.12 = (f32[4,1920]{1,0:T(4,128)S(1)}, f32[4,1920]{1,0:T(4,128)S(1)}, u32[]{:S(2)}, u32[]{:S(2)}) collective-permute-start(f32[4,1920]{1,0:T(4,128)S(1)} %get-tuple-element.29), channel_id=1, source_target_pairs={{0,4},{1,5},{2,6},{3,7},{4,0},{5,1},{6,2},{7,3},{8,12},{9,13},{10,... | collective-permute-start | bytes 92168 | tf_op jit(solution)/shard_map/ppermute | solution.py:344
  38.1 3.7 %collective-permute-start.13 = (f32[2,1920]{1,0:T(2,128)S(1)}, f32[2,1920]{1,0:T(2,128)S(1)}, u32[]{:S(2)}, u32[]{:S(2)}) collective-permute-start(f32[2,1920]{1,0:T(2,128)S(1)} %get-tuple-element.31), channel_id=1, source_target_pairs={{0,2},{1,3},{2,0},{3,1},{4,6},{5,7},{6,4},{7,5},{8,10},{9,11},{10,... | collective-permute-start | bytes 46088 | tf_op jit(solution)/shard_map/ppermute | solution.py:344
  41.9 1.3 %collective-permute-start.14 = (f32[1,1920]{1,0:T(1,128)S(1)}, f32[1,1920]{1,0:T(1,128)S(1)}, u32[]{:S(2)}, u32[]{:S(2)}) collective-permute-start(f32[1,1920]{1,0:T(1,128)S(1)} %get-tuple-element.33), channel_id=1, source_target_pairs={{0,1},{1,0},{2,3},{3,2},{4,5},{5,4},{6,7},{7,6},{8,9},{9,8},{10,11... | collective-permute-start | bytes 23048 | tf_op jit(solution)/shard_map/ppermute | solution.py:344
  42.0 15.4 %collective-permute-start.3 = (bf16[97,1792]{1,0:T(8,128)(2,1)S(1)}, bf16[97,1792]{1,0:T(8,128)(2,1)S(1)}, u32[]{:S(2)}, u32[]{:S(2)}) collective-permute-start(bf16[97,1792]{1,0:T(8,128)(2,1)S(1)} %get-tuple-element.25), channel_id=1, source_target_pairs={{8,0},{24,16},{9,1},{25,17},{10,2},{26,18},{11,3},{27,19},{12,4},{... | collective-permute-start | bytes 1042952 | tf_op jit(solution)/shard_map/ppermute | solution.py:425
  43.3 14.1 %collective-permute-start.2 = (bf16[97,1792]{1,0:T(8,128)(2,1)S(1)}, bf16[97,1792]{1,0:T(8,128)(2,1)S(1)}, u32[]{:S(2)}, u32[]{:S(2)}) collective-permute-start(bf16[97,1792]{1,0:T(8,128)(2,1)S(1)} %get-tuple-element.24), channel_id=1, source_target_pairs={{0,8},{16,24},{1,9},{17,25},{2,10},{18,26},{3,11},{19,27},{4,12},{... | collective-permute-start | bytes 1042952 | tf_op jit(solution)/shard_map/ppermute | solution.py:424
  47.9 16.2 %collective-permute-start.5 = (bf16[97,1792]{1,0:T(8,128)(2,1)S(1)}, bf16[97,1792]{1,0:T(8,128)(2,1)S(1)}, u32[]{:S(2)}, u32[]{:S(2)}) collective-permute-start(bf16[97,1792]{1,0:T(8,128)(2,1)S(1)} %collective-permute-done.4), channel_id=1, source_target_pairs={{24,16},{0,8},{25,17},{1,9},{26,18},{2,10},{27,19},{3,11},{28,20},... | collective-permute-start | bytes 1042952 | tf_op jit(solution)/shard_map/ppermute | solution.py:446

commit v2 on v1

v2 whole, which is shorter than its diff:
```python
import functools

import jax
import jax.numpy as jnp
from jax import lax
from jax.experimental import pallas as pl
from jax.experimental.pallas import tpu as pltpu
from jax.sharding import PartitionSpec as P


epsilon = 1e-06
logit_scale = 100.0
lane = 128
F32 = jnp.float32
BF16 = jnp.bfloat16


def vmem(count):
    return [pl.BlockSpec(memory_space=pltpu.VMEM)] * count


def row_stats(values):
    width = values.shape[-1]
    centre = jnp.sum(values, axis=-1, keepdims=True) * (1.0 / width)
    centred = values - centre
    variance = jnp.sum(centred * centred, axis=-1, keepdims=True) * (1.0 / width)
    return centre, centred, lax.rsqrt(variance + epsilon)


def thirds(values):
    high = values.astype(BF16).astype(F32)
    rest = values - high
    middle = rest.astype(BF16).astype(F32)
    low = (rest - middle).astype(BF16).astype(F32)
    return high, middle, low


NN = (((1,), (0,)), ((), ()))
NT = (((1,), (1,)), ((), ()))


def dot(left, right, form):
    return lax.dot_general(left, right, form, preferred_element_type=F32)


def tiles_of(depth):
    width = 256 if depth % 256 == 0 else lane
    return [(start, start + width) for start in range(0, depth, width)]


def limit(mib):
    return pltpu.CompilerParams(vmem_limit_bytes=mib * 2**20)


def block_cost(rows, depth):
    return pl.CostEstimate(
        flops=2 * rows * depth * depth, bytes_accessed=2 * depth * depth, transcendentals=0
    )


def forward_rows(act, gain, weight, put):
    _, centred, inverse = row_stats(act[...].astype(F32))
    normed = (centred * inverse * gain[...]).astype(BF16)
    for low, high in tiles_of(act.shape[1]):
        mixed = dot(normed, weight[:, low:high], NN)
        put(low, high, (act[:, low:high].astype(F32) + mixed).astype(BF16))


def backward_rows(cot, saved, gain, weight, grads, put):
    depth = cot.shape[1]
    centre, _, inverse = row_stats(saved[...].astype(F32))
    total, total_unit = 0.0, 0.0
    for low, high in tiles_of(depth):
        grad = dot(cot[...], weight[low:high], NT) * gain[:, low:high]
        grads[:, low:high] = grad
        total = total + jnp.sum(grad, axis=-1, keepdims=True)
        unit = (saved[:, low:high].astype(F32) - centre) * inverse
        total_unit = total_unit + jnp.sum(grad * unit, axis=-1, keepdims=True)
    mean = total * (1.0 / depth)
    mean_unit = total_unit * (1.0 / depth)
    for low, high in tiles_of(depth):
        unit = (saved[:, low:high].astype(F32) - centre) * inverse
        block = inverse * (grads[:, low:high] - mean - unit * mean_unit)
        put(low, high, (cot[:, low:high].astype(F32) + block).astype(BF16))


def tail_rows(rows):
    return -(-(rows + lane) // lane)


def pack_rows(rows):
    return rows + -(-3 * tail_rows(rows) // 16) * 16


def pack_kernel(text_hbm, head_hbm, out, text, head, sems):
    copies = [
        pltpu.make_async_copy(text_hbm, text, sems.at[0]),
        pltpu.make_async_copy(head_hbm, head, sems.at[1]),
    ]
    for copy in copies:
        copy.start()
    for copy in copies:
        copy.wait()
    rows = head.shape[0]
    values = text[...].astype(F32)
    unit = values * lax.rsqrt(jnp.sum(values * values, axis=-1, keepdims=True) + epsilon)
    pieces = jnp.concatenate(thirds(unit) + (jnp.zeros((5, unit.shape[1]), F32),), axis=0)
    shadow = jnp.sum(dot(pieces.astype(BF16), head[...], NT), axis=0, keepdims=True)
    count = tail_rows(rows)
    shadow = jnp.concatenate([shadow, jnp.zeros((1, count * lane - rows), F32)], axis=1)
    start = lax.rem(lax.axis_index("section") * rows, lane)
    shadow = pltpu.roll(jnp.broadcast_to(shadow, (8, count * lane)), start, 1)[0:1]
    lines = [
        part[:, lane * tile : lane * (tile + 1)] for part in thirds(shadow) for tile in range(count)
    ]
    height = pack_rows(rows) - rows
    lines.append(jnp.zeros((height - len(lines), lane), F32))
    mine = pl.ds(pl.multiple_of(lax.axis_index("dp") * lane, lane), lane)
    out[:rows] = head[:, mine]
    out[rows:] = jnp.concatenate(lines, axis=0).astype(BF16)


def pack_head(text, head):
    return pl.pallas_call(
        pack_kernel,
        in_specs=[pl.BlockSpec(memory_space=pl.ANY)] * 2,
        out_specs=pl.BlockSpec(memory_space=pltpu.VMEM),
        out_shape=pltpu.VMEM((pack_rows(head.shape[0]), lane), BF16),
        scratch_shapes=[
            pltpu.VMEM(text.shape, BF16),
            pltpu.VMEM(head.shape, BF16),
            pltpu.SemaphoreType.DMA((2,)),
        ],
        compiler_params=limit(4),
        cost_estimate=pl.CostEstimate(
            flops=8 * 10**9, bytes_accessed=2 * head.size, transcendentals=0
        ),
        name="pack_head",
    )(stay(text), stay(head))


def early_kernel(act, saved, cot, gain, weight, low_out, high_out, grads):
    cut = low_out.shape[0]
    section = lax.axis_index("section")

    def put(low, high, block):
        low_out[:, low:high] = block[:cut]
        high_out[:, low:high] = block[cut:]

    @pl.when(section < 2)
    def _():
        forward_rows(act, gain, weight, put)

    @pl.when(section >= 2)
    def _():
        backward_rows(cot, saved, gain, weight, grads, put)


def stay(value):
    return pltpu.with_memory_space_constraint(value, pltpu.HBM)


def early_block(low, act, saved, cot, gain, weight):
    rows, depth = act.shape
    return pl.pallas_call(
        early_kernel,
        in_specs=vmem(5),
        out_specs=vmem(2),
        out_shape=[
            pltpu.VMEM((low, depth), BF16),
            pltpu.VMEM((rows - low, depth), BF16),
        ],
        scratch_shapes=[pltpu.VMEM((rows, depth), F32)],
        compiler_params=limit(12),
        cost_estimate=block_cost(rows, depth),
        name="early_block",
    )(act, saved, cot, gain, weight)


def later_kernel(act, saved, cot, gain, weight, hand, pooled, low_out, high_out, grads):
    rows, depth = act.shape
    rest = hand.shape[0]
    cut = rows - rest
    section = lax.axis_index("section")
    low_out[cut:] = jnp.zeros((rest - cut, depth), BF16)

    def put(low, high, block):
        low_out[:cut, low:high] = block[:cut]
        high_out[:, low:high] = block[cut:]

    def pool(low, high, block):
        pooled[:, low:high] = jnp.sum(block.astype(F32), axis=0, keepdims=True) * (1.0 / rows)

    @pl.when(section < 3)
    def _():
        pooled[...] = jnp.zeros_like(pooled)

    @pl.when(jnp.logical_or(section == 0, section == 3))
    def _():
        low_out[:cut] = jnp.zeros((cut, depth), BF16)
        high_out[...] = hand[...]

    @pl.when(section == 1)
    def _():
        backward_rows(cot, saved, gain, weight, grads, put)

    @pl.when(section == 2)
    def _():
        forward_rows(act, gain, weight, put)

    @pl.when(section == 3)
    def _():
        forward_rows(act, gain, weight, pool)


def later_block(act, saved, cot, gain, weight, hand):
    rows, depth = act.shape
    return pl.pallas_call(
        later_kernel,
        in_specs=vmem(6),
        out_specs=vmem(3),
        out_shape=[
            pltpu.VMEM((1, depth), F32),
            pltpu.VMEM(hand.shape, BF16),
            pltpu.VMEM(hand.shape, BF16),
        ],
        scratch_shapes=[pltpu.VMEM((rows, depth), F32)],
        compiler_params=limit(12),
        cost_estimate=block_cost(rows, depth),
        name="later_block",
    )(act, saved, cot, gain, weight, hand)


def slots(packs, height):
    own, near, pair = packs
    return [(3, own, 0), (2, near, 0), (1, pair, 0), (0, pair, height)]


def features_kernel(pooled, gain, label, message, standard):
    depth = pooled.shape[1]
    _, centred, inverse = row_stats(pooled[...])
    unit = centred * inverse
    standard[:, :depth] = unit
    standard[:, depth:] = jnp.broadcast_to(inverse, (1, lane))
    message[:, :depth] = (unit * gain[...]).astype(BF16).astype(F32)
    message[:, depth:] = jnp.full((1, lane), label[0], jnp.int32).astype(F32)


def features(pooled, gain, label):
    depth = pooled.shape[1]
    return pl.pallas_call(
        features_kernel,
        in_specs=vmem(2) + [pl.BlockSpec(memory_space=pltpu.SMEM)],
        out_specs=vmem(2),
        out_shape=[jax.ShapeDtypeStruct((1, depth + lane), F32)] * 2,
        compiler_params=limit(4),
        name="features",
    )(pooled, gain, label)


def text_row(packs, rows, height, depth):
    count = tail_rows(rows)
    tiles = [jnp.zeros((1, lane), F32)] * (depth // lane + count)
    for section, pack, base in slots(packs, height):
        tail = pack[base + rows : base + height].astype(F32)
        for tile in range(count):
            place = section * rows // lane + tile
            tiles[place] = tiles[place] + sum(
                tail[part * count + tile : part * count + tile + 1] for part in range(3)
            )
    return jnp.concatenate(tiles[: depth // lane], axis=1)


def embed_kernel(rows, height, depth, table, *refs):
    packs, (keep, send, column) = refs[:-3], refs[-3:]
    count = table.shape[0]
    half = count // 2
    for section, pack, base in slots(packs, height):
        column[section * rows : (section + 1) * rows] = pack[base : base + rows]
    weight = column[...]
    embedding = dot(table[:, :depth].astype(BF16), weight, NN)
    pieces = jnp.concatenate(thirds(embedding), axis=0).astype(BF16)
    product = dot(pieces, weight, NT)
    product = product[:count] + product[count : 2 * count] + product[2 * count :]
    square = jnp.sum(embedding * embedding, axis=-1, keepdims=True)
    place = lax.broadcasted_iota(jnp.int32, (count, lane), 0)
    across = lax.broadcasted_iota(jnp.int32, (count, lane), 1)
    square = jnp.sum(jnp.where(place == across, square, 0.0), axis=0, keepdims=True)
    text = text_row(packs, rows, height, depth)
    for out, part in ((keep, product[:half]), (send, product[half:])):
        out[:half, :depth] = part
        out[half:, :depth] = text
        out[:, depth:] = jnp.broadcast_to(square, (half + 1, lane))


def embed(table, packs, rows):
    count, width = table.shape
    depth = width - lane
    return pl.pallas_call(
        functools.partial(embed_kernel, rows, pack_rows(rows), depth),
        in_specs=vmem(1 + len(packs)),
        out_specs=vmem(2),
        out_shape=[jax.ShapeDtypeStruct((count // 2 + 1, width), F32)] * 2,
        scratch_shapes=[pltpu.VMEM((depth, lane), BF16)],
        compiler_params=limit(4),
        name="embed",
    )(table, *packs)


def swapped(square, bit):
    across = lax.broadcasted_iota(jnp.int32, square.shape, 1)
    width = square.shape[1]
    up = pltpu.roll(square, bit, 1)
    down = pltpu.roll(square, width - bit, 1)
    return jnp.where((across & bit) == 0, down, up)


def fold_kernel(bit, depth, count, mine, theirs, keep, send):
    half = count // 2
    total = mine[:count, :depth] + theirs[:count, :depth]
    square = jnp.broadcast_to(mine[0:1, depth:], (8, lane)) + swapped(
        jnp.broadcast_to(theirs[0:1, depth:], (8, lane)), bit
    )
    texts = jnp.concatenate([mine[count:, :depth], theirs[count:, :depth]], axis=0)
    for out, part in ((keep, total[:half]), (send, total[half:])):
        out[:half, :depth] = part
        out[half:, :depth] = texts
        out[:, depth:] = square[: out.shape[0]]


def fold(mine, theirs, bit, count):
    rows, width = mine.shape
    after = jax.ShapeDtypeStruct((count // 2 + 2 * (rows - count), width), F32)
    return pl.pallas_call(
        functools.partial(fold_kernel, bit, width - lane, count),
        in_specs=vmem(2),
        out_specs=vmem(2),
        out_shape=[after, after],
        compiler_params=limit(4),
        name="fold",
    )(mine, theirs)


def text_order(count):
    order, bit = [0], count // 2
    while bit:
        order += [slot ^ bit for slot in order]
        bit //= 2
    return order


def loss_kernel(depth, tokens, mine, theirs, table, standard, gain, grad, loss):
    count = table.shape[0]
    half = count // 2
    order = text_order(count)
    found = [(mine, 1 + order.index(slot)) for slot in range(count)]
    found = [(ref, row) if row <= half else (theirs, row - half) for ref, row in found]
    texts = jnp.concatenate([ref[row : row + 1, :depth] for ref, row in found], axis=0)
    pieces = jnp.concatenate(thirds(texts), axis=0).astype(BF16)
    score = dot(table[:, :depth].astype(BF16), pieces, NT)
    score = score[:, :count] + score[:, count : 2 * count] + score[:, 2 * count :]
    scores = jnp.concatenate([score, jnp.zeros((count, lane - count), F32)], axis=1)
    shape = (count, lane)
    place = lax.broadcasted_iota(jnp.int32, shape, 0)
    across = lax.broadcasted_iota(jnp.int32, shape, 1)
    same = place == across
    inside = across < count
    square = jnp.broadcast_to(mine[0:1, depth:], (8, lane)) + swapped(
        jnp.broadcast_to(theirs[0:1, depth:], (8, lane)), 1
    )
    square = jnp.broadcast_to(square[0:1], shape)
    inverse = lax.rsqrt(jnp.sum(jnp.where(same, square, 0.0), axis=1, keepdims=True) + epsilon)
    logits = logit_scale * inverse * scores
    owner = (across ^ lax.axis_index("dp")).astype(F32)
    targets = jnp.where(inside & (table[:, depth : depth + 1] == owner), 1.0, 0.0)
    masked = jnp.where(inside, logits, -jnp.inf)
    row_max = jnp.max(masked, axis=1, keepdims=True)
    row_lse = row_max + jnp.log(
        jnp.sum(jnp.where(inside, jnp.exp(masked - row_max), 0.0), axis=1, keepdims=True)
    )
    col_max = jnp.max(logits, axis=0, keepdims=True)
    col_lse = col_max + jnp.log(jnp.sum(jnp.exp(logits - col_max), axis=0, keepdims=True))
    picked = jnp.sum(logits * targets, axis=1, keepdims=True)
    col_picked = jnp.sum(col_lse * targets, axis=1, keepdims=True)
    value = 0.5 / count * jnp.sum((row_lse - picked) + (col_picked - picked), axis=0, keepdims=True)
    loss[...] = jnp.broadcast_to(value, loss.shape)
    row_prob = jnp.where(inside, jnp.exp(masked - row_lse), 0.0)
    col_prob = jnp.where(inside, jnp.exp(logits - col_lse), 0.0)
    d_logits = (0.5 * (row_prob - targets + (col_prob - targets)))[0:1]
    own_inverse = inverse[0:1]
    along = jnp.sum(d_logits * logits[0:1], axis=1, keepdims=True)
    weight = jnp.sum(
        jnp.where(same, jnp.broadcast_to(d_logits, shape), 0.0), axis=1, keepdims=True
    )
    d_text = jnp.sum(weight * texts, axis=0, keepdims=True)
    product = mine[0:1, :depth] + theirs[0:1, :depth]
    d_normed = own_inverse * (logit_scale * d_text - along * own_inverse * product)
    d_unit = d_normed * gain[...]
    unit = standard[:, :depth]
    scale = 1.0 / depth
    mean = jnp.sum(d_unit, axis=1, keepdims=True) * scale
    mean_unit = jnp.sum(d_unit * unit, axis=1, keepdims=True) * scale
    grad[...] = standard[:, depth : depth + 1] * (d_unit - mean - unit * mean_unit) * (1.0 / tokens)


def loss_step(mine, theirs, table, standard, gain, tokens):
    depth = gain.shape[1]
    return pl.pallas_call(
        functools.partial(loss_kernel, depth, tokens),
        in_specs=vmem(5),
        out_specs=vmem(2),
        out_shape=[
            jax.ShapeDtypeStruct((1, depth), F32),
            jax.ShapeDtypeStruct((1, lane), F32),
        ],
        compiler_params=limit(4),
        name="loss_step",
    )(mine, theirs, table, standard, gain)


def choose_kernel(arrived, own, out):
    section = lax.axis_index("section")
    middle = jnp.logical_or(section == 1, section == 2)

    @pl.when(middle)
    def _():
        out[...] = own[...]

    @pl.when(jnp.logical_not(middle))
    def _():
        out[...] = arrived[...]


def near(value):
    return pltpu.with_memory_space_constraint(value, pltpu.VMEM)


def stack_kernel(first, second, out):
    rows = first.shape[0]
    out[:rows] = first[...]
    out[rows:] = second[...]


def stack(first, second):
    rows, width = first.shape
    return pl.pallas_call(
        stack_kernel,
        in_specs=vmem(2),
        out_specs=pl.BlockSpec(memory_space=pltpu.VMEM),
        out_shape=pltpu.VMEM((2 * rows, width), first.dtype),
        compiler_params=limit(4),
        name="stack",
    )(near(first), near(second))


def choose(arrived, own):
    return pl.pallas_call(
        choose_kernel,
        in_specs=vmem(2),
        out_specs=pl.BlockSpec(memory_space=pltpu.VMEM),
        out_shape=pltpu.VMEM(own.shape, BF16),
        compiler_params=limit(4),
        name="choose",
    )(near(arrived), near(own))


def put_rows(plan, parts, outs, sems, more):
    for section, moves in enumerate(plan):

        @pl.when(lax.axis_index("section") == section)
        def _(section=section, moves=moves):
            copies = []

            def copy(source, target):
                copies.append(pltpu.make_async_copy(source, target, sems.at[len(copies)]))
                copies[-1].start()

            for name, count, out, start in moves:
                copy(parts[name].at[pl.ds(0, count)], outs[out].at[pl.ds(start, count)])
            more(section, copy)
            for one in copies:
                one.wait()


def gather_kernel(plan, *refs):
    parts, (next_act, next_grad, zeros, sems) = refs[:-4], refs[-4:]

    def more(section, copy):
        if section == 0:
            zeros[...] = jnp.zeros_like(zeros)
            copy(zeros, next_act)

    put_rows(plan, parts, (next_act, next_grad), sems, more)


def gather_rows(plan, parts, tokens):
    depth = parts[0].shape[1]
    hbm = pl.BlockSpec(memory_space=pltpu.HBM)
    return pl.pallas_call(
        functools.partial(gather_kernel, plan),
        in_specs=vmem(len(parts)),
        out_specs=[hbm, hbm],
        out_shape=[pltpu.HBM((tokens, depth), BF16)] * 2,
        scratch_shapes=[pltpu.VMEM((tokens, depth), BF16), pltpu.SemaphoreType.DMA((4,))],
        compiler_params=limit(6),
        name="gather_rows",
    )(*(near(part) for part in parts))


def last_kernel(plan, *refs):
    parts, refs = refs[:2], refs[2:]
    grad, loss, _, _, next_act, next_grad, mean_loss, wide, sems = refs
    last = len(plan) - 1
    mean_loss[...] = jnp.where(lax.axis_index("section") == last, loss[...], 0.0)

    def more(section, copy):
        if section == last:
            wide[...] = jnp.broadcast_to(grad[...], wide.shape).astype(BF16)
            copy(wide, next_grad)

    put_rows(plan, parts, (next_act, next_grad), sems, more)


def last_rows(plan, parts, grad, loss, next_act, next_grad):
    hbm = pl.BlockSpec(memory_space=pltpu.HBM)
    return pl.pallas_call(
        functools.partial(last_kernel, plan),
        in_specs=vmem(4) + [hbm, hbm],
        out_specs=[hbm, hbm] + vmem(1),
        out_shape=[pltpu.HBM(next_act.shape, BF16)] * 2 + [jax.ShapeDtypeStruct((1, lane), F32)],
        input_output_aliases={4: 0, 5: 1},
        scratch_shapes=[pltpu.VMEM(next_act.shape, BF16), pltpu.SemaphoreType.DMA((4,))],
        compiler_params=limit(6),
        name="last_rows",
    )(near(parts[0]), near(parts[1]), near(grad), loss, next_act, next_grad)


def swap(value, axis, bit):
    count = lax.axis_size(axis)
    return lax.ppermute(value, axis, [(index, index ^ bit) for index in range(count)])


def local(
    activations,
    saved,
    cotangents,
    projection,
    section_gain,
    final_gain,
    head_weight,
    text_embed,
    labels,
):
    devices = lax.axis_size("dp")
    _, _, tokens, depth = activations.shape
    rows = head_weight.shape[0]
    act, kept, cot = (value.reshape(tokens, depth) for value in (activations, saved, cotangents))
    low = lane
    high = tokens - low
    weight = projection[0]

    pack = pack_head(text_embed, head_weight)
    other = swap(pack, "section", 1)
    send_one, hand = early_block(low, act, kept, cot, section_gain, weight)
    one = swap(send_one, "section", 1)
    hand_high = swap(hand, "section", 2)
    pooled, send_three, send_two = later_block(act, kept, cot, section_gain, weight, hand)
    two = swap(send_two, "section", 1)
    pair = swap(stack(pack, other), "section", 2)
    packs = (pack, other, pair)

    gain = final_gain.reshape(1, depth)
    table, standard = features(pooled, gain, labels)
    bit = 1
    while bit < devices:
        other = swap(table, "dp", bit)
        table = jnp.concatenate([table, other], axis=0)
        bit *= 2
    hand_low = swap(one, "section", 2)
    three = swap(choose(hand_high, send_three), "section", 1)
    mine, send = embed(table, packs, rows)
    bit = devices // 2
    while bit > 1:
        other = swap(send, "dp", bit)
        mine, send = fold(mine, other, bit, bit)
        bit //= 2
    other = swap(send, "dp", 1)
    grad, loss = loss_step(mine, other, table, standard, gain, tokens)
    plan = (
        ((1, high, 1, low),),
        ((0, low, 0, 0), (1, high, 0, low)),
        ((0, low, 1, 0), (1, high, 1, low)),
        ((1, high, 0, low),),
    )
    next_act, next_grad = gather_rows(plan, (one, two), tokens)
    plan = (
        ((0, low, 1, 0),),
        ((1, low, 1, 0), (0, high, 1, low)),
        ((1, low, 0, 0), (0, high, 0, low)),
        ((0, low, 0, 0),),
    )
    next_act, next_grad, mean_loss = last_rows(
        plan, (three, hand_low), grad, loss, next_act, next_grad
    )
    return (next_act[None, None], next_grad[None, None], mean_loss[0, 0:1])


def shifted(value, axis, steps):
    count = lax.axis_size(axis)
    first, last = (max(0, -steps), min(count, count - steps))
    return lax.ppermute(value, axis, [(source, source + steps) for source in range(first, last)])


def spread(block, axis, owner):
    block = jnp.where(lax.axis_index(axis) == owner, block, jnp.zeros_like(block))
    return lax.psum(block, axis)


def norm_rows(values):
    centre = jnp.mean(values, axis=-1, keepdims=True)
    centred = values - centre
    variance = jnp.mean(centred * centred, axis=-1, keepdims=True)
    inverse = lax.rsqrt(variance + epsilon)
    return (centred * inverse, inverse)


def unit_rows(values):
    inverse = lax.rsqrt(jnp.sum(values * values, axis=-1, keepdims=True) + epsilon)
    return (values * inverse, inverse)


def plain_forward(block_in, weight, scale_row):
    block_shape = block_in.shape
    standard, _ = norm_rows(block_in.astype(jnp.float32))
    normed = (standard * scale_row).astype(jnp.bfloat16)
    mixed = jnp.dot(normed.reshape(-1, block_shape[-1]), weight, preferred_element_type=jnp.float32)
    return (block_in.astype(jnp.float32) + mixed.reshape(block_shape)).astype(jnp.bfloat16)


def plain_backward(cotangent, restored, weight, scale_row):
    block_shape = restored.shape
    standard, inverse = norm_rows(restored.astype(jnp.float32))
    d_normed = lax.dot_general(
        cotangent.reshape(-1, block_shape[-1]),
        weight,
        (((1,), (1,)), ((), ())),
        preferred_element_type=jnp.float32,
    ).reshape(block_shape)
    d_standard = d_normed * scale_row
    d_input = cotangent.astype(jnp.float32) + inverse * (
        d_standard
        - jnp.mean(d_standard, axis=-1, keepdims=True)
        - standard * jnp.mean(d_standard * standard, axis=-1, keepdims=True)
    )
    return d_input.astype(jnp.bfloat16)


def contrastive(logits, label_values):
    count = logits.shape[0]
    targets = (label_values[:, None] == jnp.arange(count).astype(jnp.float32)[None, :]).astype(
        jnp.float32
    )
    row_lse = jax.nn.logsumexp(logits, axis=1)
    col_lse = jax.nn.logsumexp(logits, axis=0)
    picked = jnp.sum(logits * targets, axis=1)
    col_picked = jnp.sum(col_lse[None, :] * targets, axis=1)
    loss_value = 0.5 * jnp.mean(row_lse - picked) + 0.5 * jnp.mean(col_picked - picked)
    row_prob = jnp.exp(logits - row_lse[:, None])
    col_prob = jnp.exp(logits - col_lse[None, :])
    d_logits = 0.5 * (row_prob - targets + (col_prob - targets))
    return (loss_value, d_logits)


def plain_local(
    activations,
    saved,
    cotangents,
    projection,
    section_gain,
    final_gain,
    head_weight,
    text_embed,
    labels,
):
    sections = lax.axis_size("section")
    section_index = lax.axis_index("section")
    is_last = section_index == sections - 1
    weight = projection[0]
    scale_row = section_gain[0]
    incoming = activations[0]
    block_out = plain_forward(incoming, weight, scale_row)
    next_act = shifted(block_out[None], "section", 1)
    d_input = plain_backward(cotangents[0], saved[0], weight, scale_row)
    passed_grad = shifted(d_input[None], "section", -1)
    pooled = jnp.mean(block_out.astype(jnp.float32), axis=1)
    pooled_std, pooled_inv = norm_rows(pooled)
    pooled_norm = (pooled_std * final_gain).astype(jnp.bfloat16)
    shared = spread(pooled_norm, "section", sections - 1)
    row_count = head_weight.shape[0]
    my_columns = lax.dynamic_slice_in_dim(shared, section_index * row_count, row_count, 1)
    embedding = lax.psum(
        jnp.dot(my_columns, head_weight, preferred_element_type=jnp.float32), "section"
    )
    image_unit, image_inv = unit_rows(embedding)
    own_count = image_unit.shape[0]
    text_unit, _ = unit_rows(text_embed.astype(jnp.float32))
    all_image, all_text, all_labels = (
        lax.all_gather(image_unit, "dp", axis=0, tiled=True),
        lax.all_gather(text_unit, "dp", axis=0, tiled=True),
        lax.all_gather(labels.astype(jnp.float32), "dp", axis=0, tiled=True),
    )
    logits = logit_scale * jnp.dot(all_image, all_text.T, precision=lax.Precision.HIGHEST)
    loss_value, d_logits = contrastive(logits, all_labels)
    own_rows = lax.dynamic_slice_in_dim(d_logits, lax.axis_index("dp") * own_count, own_count, 0)
    d_image = logit_scale * jnp.dot(own_rows, all_text, precision=lax.Precision.HIGHEST)
    d_embedding = (
        (d_image - image_unit * jnp.sum(d_image * image_unit, axis=-1, keepdims=True)) * image_inv
    ).astype(jnp.bfloat16)
    partial_value = lax.dot_general(
        d_embedding, head_weight, (((1,), (1,)), ((), ())), preferred_element_type=jnp.float32
    )
    d_pooled_norm = lax.all_gather(partial_value, "section", axis=1, tiled=True)
    d_std = d_pooled_norm * final_gain
    d_pooled = pooled_inv * (
        d_std
        - jnp.mean(d_std, axis=-1, keepdims=True)
        - pooled_std * jnp.mean(d_std * pooled_std, axis=-1, keepdims=True)
    )
    token_count = block_out.shape[1]
    loss_grad = jnp.broadcast_to((d_pooled / token_count)[:, None, :], block_out.shape).astype(
        jnp.bfloat16
    )
    next_grad = jnp.where(is_last, loss_grad[None], passed_grad)
    mean_loss = jnp.where(is_last, loss_value, jnp.float32(0.0))[None]
    return (next_act, next_grad, mean_loss)


def fits(mesh, width):
    sections, devices = mesh.shape["section"], mesh.shape["dp"]
    power = devices > 1 and not (devices & (devices - 1))
    return sections == 4 and power and width == devices * lane


def either(mesh, *args):
    if fits(mesh, args[7].shape[1]):
        return local(*args)
    return plain_local(*args)


def solution(mesh):
    return jax.shard_map(
        functools.partial(either, mesh),
        mesh=mesh,
        in_specs=(
            P("section", "dp", None, None),
            P("section", "dp", None, None),
            P("section", "dp", None, None),
            P("section", None, None),
            P("section", None),
            P(),
            P("section", None),
            P("dp", None),
            P("dp"),
        ),
        out_specs=(P("section", "dp", None, None), P("section", "dp", None, None), P("section")),
        check_vma=False,
    )
```

time: 66.2 us -> 60.8 us (0.918)
  waiting for transfers between devices: 26.3 us -> 20.9 us
  local copies, waits for them, and re-layouts: 2.63 us -> 7.78 us
  starting transfers between devices: 26 us -> 22 us
  Pallas kernels: 9.27 us -> 8.22 us
    ppermute x15 -> x13, waiting for transfers between devices: 26.3 us -> 20.9 us  [swap(): lax.ppermute(value, axis, [(index, index ^ bit) for index in range(count)])]
    unnamed x16 -> x10, local copies, waits for them, and re-layouts: 2.62 us -> 7.08 us
    ppermute x15 -> x13, starting transfers between devices: 26 us -> 22 us  [swap(): lax.ppermute(value, axis, [(index, index ^ bit) for index in range(count)])]
    pallas_call x8 -> x11, Pallas kernels: 8.72 us -> 7.59 us  [the longest x1 2.46 us: early_block(): pl.pallas_call(early_kernel, in_specs=vmem(5), out_specs=vmem(2), out_sha...]
    reshape x1, local copies, waits for them, and re-layouts: 0.01 us -> 0.7 us  [local(): gain = final_gain.reshape(1, depth)]
  transfers between devices with their start and end apart: 15 -> 13, of which waited for: 6 -> 6; matrix products, arithmetic and copies ran while one was open for 0% -> 0% of each run, Pallas kernels for 10% -> 7%
where the time goes in v2:
time: 60.8 us; the launch traced here: 60.4 us
  starting transfers between devices  22 us (36%)
  waiting for transfers between devices  20.9 us (34%)
  Pallas kernels  8.22 us (14%)
  local copies, waits for them, and re-layouts  7.78 us (13%)
  between operations  1.39 us (2%)
    ppermute x13, starting transfers between devices, swap(): lax.ppermute(value, axis, [(index, index ^ bit) for index in range(count)])  22 us
    ppermute x13, waiting for transfers between devices, swap(): lax.ppermute(value, axis, [(index, index ^ bit) for index in range(count)])  20.9 us
    unnamed x10, local copies, waits for them, and re-layouts  7.08 us
    pallas_call x1, Pallas kernels, early_block(): pl.pallas_call(early_kernel, in_specs=vmem(5), out_specs=vmem(2), out_sha...  2.46 us
    pallas_call x1, Pallas kernels, pack_head(): pl.pallas_call(pack_kernel, in_specs=[pl.BlockSpec(memory_space=pl.ANY)]...  1.73 us
    pallas_call x1, Pallas kernels, last_rows(): pl.pallas_call(functools.partial(last_kernel, plan), in_specs=vmem(4) + [...  1.33 us
  transfers between devices with their start and end apart: 13, of which 6 were waited for; matrix products, arithmetic and copies ran while one was open for 0% of the time, Pallas kernels for 7%

profile of v2, /device:TPU:0, one launch (start us, length us, event | category | flops | bytes accessed | tf_op | source)
XLA Modules:
  0.0 60.4 jit_solution(16017221447300964896)
XLA Ops:
  1.3 0.7 %reshape.21.gain = f32[1,1792]{1,0:T(1,128)S(1)} reshape(f32[1792]{0:T(1024)} %param.14) | data formatting | bytes 14336 | tf_op jit(solution)/shard_map/reshape | solution.py:572
  2.0 2.8 %copy-done = bf16[1,1792,1792]{2,1,0:T(8,128)(2,1)S(1)} copy-done((bf16[1,1792,1792]{2,1,0:T(8,128)(2,1)S(1)}, bf16[1,1792,1792]{2,1,0:T(8,128)(2,1)}, u32[]{:S(2)}) %copy-start) | copy-done | bytes 6422552
  4.8 1.2 %copy-done.1 = bf16[1,1,257,1792]{3,2,1,0:T(8,128)(2,1)S(1)} copy-done((bf16[1,1,257,1792]{3,2,1,0:T(8,128)(2,1)S(1)}, bf16[1,1,257,1792]{3,2,1,0:T(8,128)(2,1)}, u32[]{:S(2)}) %copy-start.1) | copy-done | bytes 921112
  6.0 1.2 %copy-done.2 = bf16[1,1,257,1792]{3,2,1,0:T(8,128)(2,1)S(1)} copy-done((bf16[1,1,257,1792]{3,2,1,0:T(8,128)(2,1)S(1)}, bf16[1,1,257,1792]{3,2,1,0:T(8,128)(2,1)}, u32[]{:S(2)}) %copy-start.2) | copy-done | bytes 921112
  7.2 1.2 %copy-done.3 = bf16[1,1,257,1792]{3,2,1,0:T(8,128)(2,1)S(1)} copy-done((bf16[1,1,257,1792]{3,2,1,0:T(8,128)(2,1)S(1)}, bf16[1,1,257,1792]{3,2,1,0:T(8,128)(2,1)}, u32[]{:S(2)}) %copy-start.3) | copy-done | bytes 921112
  8.4 0.7 %copy-done.4 = f32[1,1792]{1,0:T(1,128)S(1)} copy-done((f32[1,1792]{1,0:T(1,128)S(1)}, f32[1,1792]{1,0:T(1,128)}, u32[]{:S(2)}) %copy-start.4) | copy-done | bytes 7192
  9.1 2.5 %early_block.1 = (bf16[128,1792]{1,0:T(8,128)(2,1)S(1)}, bf16[129,1792]{1,0:T(8,128)(2,1)S(1)}) custom-call(bf16[257,1792]{1,0:T(8,128)(2,1)S(1)} %bitcast.10, bf16[257,1792]{1,0:T(8,128)(2,1)S(1)} %bitcast.12, bf16[257,1792]{1,0:T(8,128)(2,1)S(1)} %bitcast.14, f32[1,1792]{1,0:T(1,128)S(1)} %copy-done.4, bf16[1792,1792]{1,0:T(8,128)(2,1)S(1)} %bitcast.8), custom_call_target="tpu_custom_call" | custom-call | flops 1650589696 | bytes 6422528 | tf_op jit(solution)/shard_map/early_block/pallas_call | solution.py:165
  11.5 0.1 later_block.1
  11.6 0.2 features.1
  11.8 0.6 collective-permute-start.4
  12.4 5.6 %collective-permute-start = (bf16[129,1792]{1,0:T(8,128)(2,1)S(1)}, bf16[129,1792]{1,0:T(8,128)(2,1)S(1)}, u32[]{:S(2)}, u32[]{:S(2)}) collective-permute-start(bf16[129,1792]{1,0:T(8,128)(2,1)S(1)} %get-tuple-element.23.hand), channel_id=1, source_target_pairs={{0,16},{8,24},{16,0},{24,8},{1,17},{9,25},{17,1},{25,9},{2,18},{10... | collective-permute-start | bytes 1387016 | tf_op jit(solution)/shard_map/ppermute | solution.py:540
  18.0 1.6 %collective-permute-start.2 = (bf16[128,1792]{1,0:T(8,128)(2,1)S(1)}, bf16[128,1792]{1,0:T(8,128)(2,1)S(1)}, u32[]{:S(2)}, u32[]{:S(2)}) collective-permute-start(bf16[128,1792]{1,0:T(8,128)(2,1)S(1)} %get-tuple-element.25), channel_id=1, source_target_pairs={{0,8},{8,0},{16,24},{24,16},{1,9},{9,1},{17,25},{25,17},{2,10},{10... | collective-permute-start | bytes 1376264 | tf_op jit(solution)/shard_map/ppermute | solution.py:540
  19.6 1.6 %collective-permute-start.5 = (f32[2,1920]{1,0:T(2,128)S(1)}, f32[2,1920]{1,0:T(2,128)S(1)}, u32[]{:S(2)}, u32[]{:S(2)}) collective-permute-start(f32[2,1920]{1,0:T(2,128)S(1)} %pad_maximum_fusion.2), channel_id=1, source_target_pairs={{0,2},{1,3},{2,0},{3,1},{4,6},{5,7},{6,4},{7,5},{8,10},{9,11},{10,... | collective-permute-start | bytes 46088 | tf_op jit(solution)/shard_map/ppermute | solution.py:540
  21.2 1.7 %pack_head.1.first.refs_0_ = bf16[464,128]{1,0:T(8,128)(2,1)S(1)} custom-call(bf16[1,1024]{1,0:T(2,128)(2,1)} %text_hbm.1, bf16[448,1024]{1,0:T(8,128)(2,1)} %head_hbm.1), custom_call_target="tpu_custom_call" | custom-call | flops 8000000000 | bytes 917504 | tf_op jit(solution)/shard_map/pack_head/pallas_call | solution.py:124
  22.9 0.5 collective-permute-start.7
  23.5 1.6 %collective-permute-start.12 = (bf16[129,1792]{1,0:T(8,128)(2,1)S(1)}, bf16[129,1792]{1,0:T(8,128)(2,1)S(1)}, u32[]{:S(2)}, u32[]{:S(2)}) collective-permute-start(bf16[129,1792]{1,0:T(8,128)(2,1)S(1)} %get-tuple-element.37), channel_id=1, source_target_pairs={{0,8},{8,0},{16,24},{24,16},{1,9},{9,1},{17,25},{25,17},{2,10},{10... | collective-permute-start | bytes 1387016 | tf_op jit(solution)/shard_map/ppermute | solution.py:540
  25.0 6.3 %collective-permute-done.2.refs_0_ = bf16[128,1792]{1,0:T(8,128)(2,1)S(1)} collective-permute-done((bf16[128,1792]{1,0:T(8,128)(2,1)S(1)}, bf16[128,1792]{1,0:T(8,128)(2,1)S(1)}, u32[]{:S(2)}, u32[]{:S(2)}) %collective-permute-start.2) | collective-permute-done | bytes 458784 | tf_op jit(solution)/shard_map/ppermute | solution.py:540
  31.4 0.1 collective-permute-start.3
  31.5 2.0 %collective-permute-start.1 = (bf16[129,1792]{1,0:T(8,128)(2,1)S(1)}, bf16[129,1792]{1,0:T(8,128)(2,1)S(1)}, u32[]{:S(2)}, u32[]{:S(2)}) collective-permute-start(bf16[129,1792]{1,0:T(8,128)(2,1)S(1)} %choose.1), channel_id=1, source_target_pairs={{0,8},{8,0},{16,24},{24,16},{1,9},{9,1},{17,25},{25,17},{2,10},{10... | collective-permute-start | bytes 1387016 | tf_op jit(solution)/shard_map/ppermute | solution.py:540
  33.5 2.7 %collective-permute-start.6 = (f32[4,1920]{1,0:T(4,128)S(1)}, f32[4,1920]{1,0:T(4,128)S(1)}, u32[]{:S(2)}, u32[]{:S(2)}) collective-permute-start(f32[4,1920]{1,0:T(4,128)S(1)} %pad_maximum_fusion.1), channel_id=1, source_target_pairs={{0,4},{1,5},{2,6},{3,7},{4,0},{5,1},{6,2},{7,3},{8,12},{9,13},{10,... | collective-permute-start | bytes 92168 | tf_op jit(solution)/shard_map/ppermute | solution.py:540
  36.2 1.7 %collective-permute-start.8 = (bf16[928,128]{1,0:T(8,128)(2,1)S(1)}, bf16[928,128]{1,0:T(8,128)(2,1)S(1)}, u32[]{:S(2)}, u32[]{:S(2)}) collective-permute-start(bf16[928,128]{1,0:T(8,128)(2,1)S(1)} %stack.1), channel_id=1, source_target_pairs={{0,16},{8,24},{16,0},{24,8},{1,17},{9,25},{17,1},{25,9},{2,18},{10... | collective-permute-start | bytes 712712 | tf_op jit(solution)/shard_map/ppermute | solution.py:540
  37.8 0.5 collective-permute-done.6
  38.4 9.0 %collective-permute-done.8.refs_2_ = bf16[928,128]{1,0:T(8,128)(2,1)S(1)} collective-permute-done((bf16[928,128]{1,0:T(8,128)(2,1)S(1)}, bf16[928,128]{1,0:T(8,128)(2,1)S(1)}, u32[]{:S(2)}, u32[]{:S(2)}) %collective-permute-start.8) | collective-permute-done | bytes 237600 | tf_op jit(solution)/shard_map/ppermute | solution.py:540
  47.3 0.4 embed.1
  47.8 2.6 %collective-permute-start.9 = (f32[5,1920]{1,0:T(8,128)S(1)}, f32[5,1920]{1,0:T(8,128)S(1)}, u32[]{:S(2)}, u32[]{:S(2)}) collective-permute-start(f32[5,1920]{1,0:T(8,128)S(1)} %get-tuple-element.29), channel_id=1, source_target_pairs={{0,4},{1,5},{2,6},{3,7},{4,0},{5,1},{6,2},{7,3},{8,12},{9,13},{10,... | collective-permute-start | bytes 115208 | tf_op jit(solution)/shard_map/ppermute | solution.py:540
  50.4 2.6 %collective-permute-done.9.theirs = f32[5,1920]{1,0:T(8,128)S(1)} collective-permute-done((f32[5,1920]{1,0:T(8,128)S(1)}, f32[5,1920]{1,0:T(8,128)S(1)}, u32[]{:S(2)}, u32[]{:S(2)}) %collective-permute-start.9) | collective-permute-done | bytes 38432 | tf_op jit(solution)/shard_map/ppermute | solution.py:540
  53.1 1.5 %collective-permute-start.10 = (f32[4,1920]{1,0:T(4,128)S(1)}, f32[4,1920]{1,0:T(4,128)S(1)}, u32[]{:S(2)}, u32[]{:S(2)}) collective-permute-start(f32[4,1920]{1,0:T(4,128)S(1)} %get-tuple-element.31), channel_id=1, source_target_pairs={{0,2},{1,3},{2,0},{3,1},{4,6},{5,7},{6,4},{7,5},{8,10},{9,11},{10,... | collective-permute-start | bytes 92168 | tf_op jit(solution)/shard_map/ppermute | solution.py:540
  54.6 2.4 %collective-permute-done.10.theirs = f32[4,1920]{1,0:T(4,128)S(1)} collective-permute-done((f32[4,1920]{1,0:T(4,128)S(1)}, f32[4,1920]{1,0:T(4,128)S(1)}, u32[]{:S(2)}, u32[]{:S(2)}) %collective-permute-start.10) | collective-permute-done | bytes 30752 | tf_op jit(solution)/shard_map/ppermute | solution.py:540
  57.2 1.1 %gather_rows.1 = (bf16[257,1792]{1,0:T(8,128)(2,1)}, bf16[257,1792]{1,0:T(8,128)(2,1)}) custom-call(bf16[128,1792]{1,0:T(8,128)(2,1)S(1)} %collective-permute-done.2.refs_0_, bf16[129,1792]{1,0:T(8,128)(2,1)S(1)} %collective-permute-done.12.refs_1_), custom_call_target="tpu_custom_call" | custom-call | tf_op jit(solution)/shard_map/gather_rows/pallas_call | solution.py:499
  58.3 0.1 collective-permute-done.11.theirs
  58.4 0.6 %loss_step.1 = (f32[1,1792]{1,0:T(1,128)S(1)}, f32[1,128]{1,0:T(1,128)S(1)}) custom-call(f32[5,1920]{1,0:T(8,128)S(1)} %get-tuple-element.32.mine, f32[5,1920]{1,0:T(8,128)S(1)} %collective-permute-done.11.theirs, f32[8,1920]{1,0:T(8,128)S(1)} %pad_maximum_fusion.table, f32[1,1920]{1,0:T(1,128)S(1)} %get-tuple-element.34.standard, f32[1,1792]{1,0:T(1,128)S(1)} %reshape.21.gain), custom_call_target="tpu_custom_call" | custom-call | tf_op jit(solution)/shard_map/loss_step/pallas_call | solution.py:408
  59.1 1.3 %last_rows.1 = (bf16[257,1792]{1,0:T(8,128)(2,1)}, bf16[257,1792]{1,0:T(8,128)(2,1)}, f32[1,128]{1,0:T(1,128)}) custom-call(bf16[129,1792]{1,0:T(8,128)(2,1)S(1)} %collective-permute-done.1.refs_0_, bf16[128,1792]{1,0:T(8,128)(2,1)S(1)} %collective-permute-done.3.refs_1_, ...), custom_call_target="tpu_custom_call", output_to_operand_aliasing={{0}: (4, {}), {1}: (5, {})} | custom-call | tf_op jit(solution)/shard_map/last_rows/pallas_call | solution.py:526
  (20 shorter events, 0.3 us)
Async XLA Ops:
  2.0 2.8 %copy-start = (bf16[1,1792,1792]{2,1,0:T(8,128)(2,1)S(1)}, bf16[1,1792,1792]{2,1,0:T(8,128)(2,1)}, u32[]{:S(2)}) copy-start(bf16[1,1792,1792]{2,1,0:T(8,128)(2,1)} %param.12) | copy-start | bytes 19267588
  4.8 1.2 %copy-start.1 = (bf16[1,1,257,1792]{3,2,1,0:T(8,128)(2,1)S(1)}, bf16[1,1,257,1792]{3,2,1,0:T(8,128)(2,1)}, u32[]{:S(2)}) copy-start(bf16[1,1,257,1792]{3,2,1,0:T(8,128)(2,1)} %param.9) | copy-start | bytes 2763268
  6.0 1.2 %copy-start.2 = (bf16[1,1,257,1792]{3,2,1,0:T(8,128)(2,1)S(1)}, bf16[1,1,257,1792]{3,2,1,0:T(8,128)(2,1)}, u32[]{:S(2)}) copy-start(bf16[1,1,257,1792]{3,2,1,0:T(8,128)(2,1)} %param.10) | copy-start | bytes 2763268
  7.2 1.2 %copy-start.3 = (bf16[1,1,257,1792]{3,2,1,0:T(8,128)(2,1)S(1)}, bf16[1,1,257,1792]{3,2,1,0:T(8,128)(2,1)}, u32[]{:S(2)}) copy-start(bf16[1,1,257,1792]{3,2,1,0:T(8,128)(2,1)} %param.11) | copy-start | bytes 2763268
  8.4 0.7 %copy-start.4 = (f32[1,1792]{1,0:T(1,128)S(1)}, f32[1,1792]{1,0:T(1,128)}, u32[]{:S(2)}) copy-start(f32[1,1792]{1,0:T(1,128)} %gain.3) | copy-start | bytes 21508
  11.8 7.7 %collective-permute-start.4 = (f32[1,1920]{1,0:T(1,128)S(1)}, f32[1,1920]{1,0:T(1,128)S(1)}, u32[]{:S(2)}, u32[]{:S(2)}) collective-permute-start(f32[1,1920]{1,0:T(1,128)S(1)} %get-tuple-element.27), channel_id=1, source_target_pairs={{0,1},{1,0},{2,3},{3,2},{4,5},{5,4},{6,7},{7,6},{8,9},{9,8},{10,11... | collective-permute-start | bytes 23048 | tf_op jit(solution)/shard_map/ppermute | solution.py:540
  12.4 19.0 %collective-permute-start = (bf16[129,1792]{1,0:T(8,128)(2,1)S(1)}, bf16[129,1792]{1,0:T(8,128)(2,1)S(1)}, u32[]{:S(2)}, u32[]{:S(2)}) collective-permute-start(bf16[129,1792]{1,0:T(8,128)(2,1)S(1)} %get-tuple-element.23.hand), channel_id=1, source_target_pairs={{0,16},{8,24},{16,0},{24,8},{1,17},{9,25},{17,1},{25,9},{2,18},{10... | collective-permute-start | bytes 1387016 | tf_op jit(solution)/shard_map/ppermute | solution.py:540
  18.0 13.4 %collective-permute-start.2 = (bf16[128,1792]{1,0:T(8,128)(2,1)S(1)}, bf16[128,1792]{1,0:T(8,128)(2,1)S(1)}, u32[]{:S(2)}, u32[]{:S(2)}) collective-permute-start(bf16[128,1792]{1,0:T(8,128)(2,1)S(1)} %get-tuple-element.25), channel_id=1, source_target_pairs={{0,8},{8,0},{16,24},{24,16},{1,9},{9,1},{17,25},{25,17},{2,10},{10... | collective-permute-start | bytes 1376264 | tf_op jit(solution)/shard_map/ppermute | solution.py:540
  19.6 13.9 %collective-permute-start.5 = (f32[2,1920]{1,0:T(2,128)S(1)}, f32[2,1920]{1,0:T(2,128)S(1)}, u32[]{:S(2)}, u32[]{:S(2)}) collective-permute-start(f32[2,1920]{1,0:T(2,128)S(1)} %pad_maximum_fusion.2), channel_id=1, source_target_pairs={{0,2},{1,3},{2,0},{3,1},{4,6},{5,7},{6,4},{7,5},{8,10},{9,11},{10,... | collective-permute-start | bytes 46088 | tf_op jit(solution)/shard_map/ppermute | solution.py:540
  22.9 13.2 %collective-permute-start.7 = (bf16[464,128]{1,0:T(8,128)(2,1)S(1)}, bf16[464,128]{1,0:T(8,128)(2,1)S(1)}, u32[]{:S(2)}, u32[]{:S(2)}) collective-permute-start(bf16[464,128]{1,0:T(8,128)(2,1)S(1)} %pack_head.1.first.refs_0_), channel_id=1, source_target_pairs={{0,8},{8,0},{16,24},{24,16},{1,9},{9,1},{17,25},{25,17},{2,10},{10... | collective-permute-start | bytes 356360 | tf_op jit(solution)/shard_map/ppermute | solution.py:540
  23.5 33.7 %collective-permute-start.12 = (bf16[129,1792]{1,0:T(8,128)(2,1)S(1)}, bf16[129,1792]{1,0:T(8,128)(2,1)S(1)}, u32[]{:S(2)}, u32[]{:S(2)}) collective-permute-start(bf16[129,1792]{1,0:T(8,128)(2,1)S(1)} %get-tuple-element.37), channel_id=1, source_target_pairs={{0,8},{8,0},{16,24},{24,16},{1,9},{9,1},{17,25},{25,17},{2,10},{10... | collective-permute-start | bytes 1387016 | tf_op jit(solution)/shard_map/ppermute | solution.py:540
  31.4 27.7 %collective-permute-start.3 = (bf16[128,1792]{1,0:T(8,128)(2,1)S(1)}, bf16[128,1792]{1,0:T(8,128)(2,1)S(1)}, u32[]{:S(2)}, u32[]{:S(2)}) collective-permute-start(bf16[128,1792]{1,0:T(8,128)(2,1)S(1)} %collective-permute-done.2.refs_0_), channel_id=1, source_target_pairs={{0,16},{8,24},{16,0},{24,8},{1,17},{9,25},{17,1},{25,9},{2,18},{10... | collective-permute-start | bytes 1376264 | tf_op jit(solution)/shard_map/ppermute | solution.py:540
  31.5 27.6 %collective-permute-start.1 = (bf16[129,1792]{1,0:T(8,128)(2,1)S(1)}, bf16[129,1792]{1,0:T(8,128)(2,1)S(1)}, u32[]{:S(2)}, u32[]{:S(2)}) collective-permute-start(bf16[129,1792]{1,0:T(8,128)(2,1)S(1)} %choose.1), channel_id=1, source_target_pairs={{0,8},{8,0},{16,24},{24,16},{1,9},{9,1},{17,25},{25,17},{2,10},{10... | collective-permute-start | bytes 1387016 | tf_op jit(solution)/shard_map/ppermute | solution.py:540
  33.5 4.9 %collective-permute-start.6 = (f32[4,1920]{1,0:T(4,128)S(1)}, f32[4,1920]{1,0:T(4,128)S(1)}, u32[]{:S(2)}, u32[]{:S(2)}) collective-permute-start(f32[4,1920]{1,0:T(4,128)S(1)} %pad_maximum_fusion.1), channel_id=1, source_target_pairs={{0,4},{1,5},{2,6},{3,7},{4,0},{5,1},{6,2},{7,3},{8,12},{9,13},{10,... | collective-permute-start | bytes 92168 | tf_op jit(solution)/shard_map/ppermute | solution.py:540
  36.2 11.2 %collective-permute-start.8 = (bf16[928,128]{1,0:T(8,128)(2,1)S(1)}, bf16[928,128]{1,0:T(8,128)(2,1)S(1)}, u32[]{:S(2)}, u32[]{:S(2)}) collective-permute-start(bf16[928,128]{1,0:T(8,128)(2,1)S(1)} %stack.1), channel_id=1, source_target_pairs={{0,16},{8,24},{16,0},{24,8},{1,17},{9,25},{17,1},{25,9},{2,18},{10... | collective-permute-start | bytes 712712 | tf_op jit(solution)/shard_map/ppermute | solution.py:540
  47.8 5.3 %collective-permute-start.9 = (f32[5,1920]{1,0:T(8,128)S(1)}, f32[5,1920]{1,0:T(8,128)S(1)}, u32[]{:S(2)}, u32[]{:S(2)}) collective-permute-start(f32[5,1920]{1,0:T(8,128)S(1)} %get-tuple-element.29), channel_id=1, source_target_pairs={{0,4},{1,5},{2,6},{3,7},{4,0},{5,1},{6,2},{7,3},{8,12},{9,13},{10,... | collective-permute-start | bytes 115208 | tf_op jit(solution)/shard_map/ppermute | solution.py:540
  53.1 3.9 %collective-permute-start.10 = (f32[4,1920]{1,0:T(4,128)S(1)}, f32[4,1920]{1,0:T(4,128)S(1)}, u32[]{:S(2)}, u32[]{:S(2)}) collective-permute-start(f32[4,1920]{1,0:T(4,128)S(1)} %get-tuple-element.31), channel_id=1, source_target_pairs={{0,2},{1,3},{2,0},{3,1},{4,6},{5,7},{6,4},{7,5},{8,10},{9,11},{10,... | collective-permute-start | bytes 92168 | tf_op jit(solution)/shard_map/ppermute | solution.py:540
  57.1 1.3 %collective-permute-start.11 = (f32[5,1920]{1,0:T(8,128)S(1)}, f32[5,1920]{1,0:T(8,128)S(1)}, u32[]{:S(2)}, u32[]{:S(2)}) collective-permute-start(f32[5,1920]{1,0:T(8,128)S(1)} %get-tuple-element.33), channel_id=1, source_target_pairs={{0,1},{1,0},{2,3},{3,2},{4,5},{5,4},{6,7},{7,6},{8,9},{9,8},{10,11... | collective-permute-start | bytes 115208 | tf_op jit(solution)/shard_map/ppermute | solution.py:540

commit v3 on v2

--- a/solution.py
+++ b/solution.py
@@ -139,36 +139,66 @@
     )(stay(text), stay(head))
 
 
+def stacked_rows(extra, depth):
+    return depth + -(-extra * depth // lane // 16) * 16
+
+
+def put_tiles(out, low, high, block):
+    for start in range(low, high, lane):
+        out[start : start + lane] = block[:, start - low : start - low + lane]
+
+
+def put_lines(out, extra, depth, pieces):
+    lines = [
+        piece[row : row + 1, start : start + lane]
+        for row in range(extra)
+        for piece in pieces
+        for start in range(0, piece.shape[1], lane)
+    ]
+    lines.append(jnp.zeros((out.shape[0] - depth - len(lines), lane), F32))
+    out[depth:] = jnp.concatenate(lines, axis=0).astype(BF16)
+
+
 def early_kernel(act, saved, cot, gain, weight, low_out, high_out, grads):
-    cut = low_out.shape[0]
+    rows, depth = act.shape
     section = lax.axis_index("section")
 
-    def put(low, high, block):
-        low_out[:, low:high] = block[:cut]
-        high_out[:, low:high] = block[cut:]
+    def putter():
+        pieces = []
+
+        def put(low, high, block):
+            low_out[:, low:high] = block[:lane]
+            put_tiles(high_out, low, high, block[lane : 2 * lane])
+            pieces.append(block[2 * lane :].astype(F32))
+
+        return pieces, put
 
     @pl.when(section < 2)
     def _():
+        pieces, put = putter()
         forward_rows(act, gain, weight, put)
+        put_lines(high_out, rows - 2 * lane, depth, pieces)
 
     @pl.when(section >= 2)
     def _():
+        pieces, put = putter()
         backward_rows(cot, saved, gain, weight, grads, put)
+        put_lines(high_out, rows - 2 * lane, depth, pieces)
 
 
 def stay(value):
     return pltpu.with_memory_space_constraint(value, pltpu.HBM)
 
 
-def early_block(low, act, saved, cot, gain, weight):
+def early_block(act, saved, cot, gain, weight):
     rows, depth = act.shape
     return pl.pallas_call(
         early_kernel,
         in_specs=vmem(5),
         out_specs=vmem(2),
         out_shape=[
-            pltpu.VMEM((low, depth), BF16),
-            pltpu.VMEM((rows - low, depth), BF16),
+            pltpu.VMEM((lane, depth), BF16),
+            pltpu.VMEM((stacked_rows(rows - 2 * lane, depth), lane), BF16),
         ],
         scratch_shapes=[pltpu.VMEM((rows, depth), F32)],
         compiler_params=limit(12),
@@ -179,14 +209,19 @@
 
 def later_kernel(act, saved, cot, gain, weight, hand, pooled, low_out, high_out, grads):
     rows, depth = act.shape
-    rest = hand.shape[0]
-    cut = rows - rest
     section = lax.axis_index("section")
-    low_out[cut:] = jnp.zeros((rest - cut, depth), BF16)
-
-    def put(low, high, block):
-        low_out[:cut, low:high] = block[:cut]
-        high_out[:, low:high] = block[cut:]
+    tail = low_out.shape[0] - depth
+    low_out[depth:] = jnp.zeros((tail, lane), BF16)
+
+    def putter():
+        pieces = []
+
+        def put(low, high, block):
+            put_tiles(low_out, low, high, block[:lane])
+            put_tiles(high_out, low, high, block[lane : 2 * lane])
+            pieces.append(block[2 * lane :].astype(F32))
+
+        return pieces, put
 
     def pool(low, high, block):
         pooled[:, low:high] = jnp.sum(block.astype(F32), axis=0, keepdims=True) * (1.0 / rows)
@@ -197,16 +232,20 @@
 
     @pl.when(jnp.logical_or(section == 0, section == 3))
     def _():
-        low_out[:cut] = jnp.zeros((cut, depth), BF16)
+        low_out[:depth] = jnp.zeros((depth, lane), BF16)
         high_out[...] = hand[...]
 
     @pl.when(section == 1)
     def _():
+        pieces, put = putter()
         backward_rows(cot, saved, gain, weight, grads, put)
+        put_lines(high_out, rows - 2 * lane, depth, pieces)
 
     @pl.when(section == 2)
     def _():
+        pieces, put = putter()
         forward_rows(act, gain, weight, put)
+        put_lines(high_out, rows - 2 * lane, depth, pieces)
 
     @pl.when(section == 3)
     def _():
@@ -271,7 +310,22 @@
     return jnp.concatenate(tiles[: depth // lane], axis=1)
 
 
-def embed_kernel(rows, height, depth, table, *refs):
+def text_kernel(rows, height, depth, *refs):
+    refs[-1][...] = text_row(refs[:-1], rows, height, depth)
+
+
+def own_text(packs, rows, depth):
+    return pl.pallas_call(
+        functools.partial(text_kernel, rows, pack_rows(rows), depth),
+        in_specs=vmem(len(packs)),
+        out_specs=pl.BlockSpec(memory_space=pltpu.VMEM),
+        out_shape=pltpu.VMEM((1, depth), F32),
+        compiler_params=limit(4),
+        name="own_text",
+    )(*(near(pack) for pack in packs))
+
+
+def embed_kernel(rows, height, depth, table, text, *refs):
     packs, (keep, send, column) = refs[:-3], refs[-3:]
     count = table.shape[0]
     half = count // 2
@@ -286,25 +340,24 @@
     place = lax.broadcasted_iota(jnp.int32, (count, lane), 0)
     across = lax.broadcasted_iota(jnp.int32, (count, lane), 1)
     square = jnp.sum(jnp.where(place == across, square, 0.0), axis=0, keepdims=True)
-    text = text_row(packs, rows, height, depth)
     for out, part in ((keep, product[:half]), (send, product[half:])):
         out[:half, :depth] = part
-        out[half:, :depth] = text
+        out[half:, :depth] = text[...]
         out[:, depth:] = jnp.broadcast_to(square, (half + 1, lane))
 
 
-def embed(table, packs, rows):
+def embed(table, text, packs, rows):
     count, width = table.shape
     depth = width - lane
     return pl.pallas_call(
         functools.partial(embed_kernel, rows, pack_rows(rows), depth),
-        in_specs=vmem(1 + len(packs)),
+        in_specs=vmem(2 + len(packs)),
         out_specs=vmem(2),
         out_shape=[jax.ShapeDtypeStruct((count // 2 + 1, width), F32)] * 2,
         scratch_shapes=[pltpu.VMEM((depth, lane), BF16)],
         compiler_params=limit(4),
         name="embed",
-    )(table, *packs)
+    )(table, text, *packs)
 
 
 def swapped(square, bit):
@@ -464,7 +517,9 @@
     )(near(arrived), near(own))
 
 
-def put_rows(plan, parts, outs, sems, more):
+def put_rows(plan, parts, outs, row, sems, more):
+    tokens, depth = outs[0].shape
+    extra = tokens - 2 * lane
     for section, moves in enumerate(plan):
 
         @pl.when(lax.axis_index("section") == section)
@@ -475,41 +530,63 @@
                 copies.append(pltpu.make_async_copy(source, target, sems.at[len(copies)]))
                 copies[-1].start()
 
-            for name, count, out, start in moves:
-                copy(parts[name].at[pl.ds(0, count)], outs[out].at[pl.ds(start, count)])
+            for name, out, start, whole in moves:
+                part, out = parts[name], outs[out]
+                if part.shape == (lane, depth):
+                    copy(part, out.at[pl.ds(start, lane)])
+                    continue
+                for place in range(0, depth, lane):
+                    copy(
+                        part.at[pl.ds(place, lane)],
+                        out.at[pl.ds(start, lane), pl.ds(place, lane)],
+                    )
+                if whole:
+                    lines = part[depth:].astype(F32)
+                    count = depth // lane
+                    line = [
+                        jnp.concatenate(
+                            [lines[at * count + tile : at * count + tile + 1] for tile in range(count)],
+                            axis=1,
+                        )
+                        for at in range(extra)
+                    ]
+                    row[16:] = jnp.concatenate(line, axis=0).astype(BF16)
+                    copy(row.at[pl.ds(16, extra)], out.at[pl.ds(start + lane, extra)])
             more(section, copy)
             for one in copies:
                 one.wait()
 
 
-def gather_kernel(plan, *refs):
-    parts, (next_act, next_grad, zeros, sems) = refs[:-4], refs[-4:]
-
+def rows_call(kernel, plan, parts, more, tokens, depth, outs=()):
+    hbm = pl.BlockSpec(memory_space=pltpu.HBM)
+    count = len(parts) + len(more)
+    extra = tokens - 2 * lane
+    loss = [jax.ShapeDtypeStruct((1, lane), F32)] if more else []
+    return pl.pallas_call(
+        functools.partial(kernel, plan),
+        in_specs=vmem(count) + [hbm] * len(outs),
+        out_specs=[hbm, hbm] + vmem(len(loss)),
+        out_shape=[pltpu.HBM((tokens, depth), BF16)] * 2 + loss,
+        input_output_aliases={count + place: place for place in range(len(outs))},
+        scratch_shapes=[
+            pltpu.VMEM((tokens, depth), BF16),
+            pltpu.VMEM((16 + extra, depth), BF16),
+            pltpu.SemaphoreType.DMA((2 * depth // lane + 4,)),
+        ],
+        compiler_params=limit(6),
+    )(*(near(part) for part in parts), *more, *outs)
+
+
+def gather_kernel(plan, one, two, next_act, next_grad, wide, row, sems):
     def more(section, copy):
         if section == 0:
-            zeros[...] = jnp.zeros_like(zeros)
-            copy(zeros, next_act)
-
-    put_rows(plan, parts, (next_act, next_grad), sems, more)
-
-
-def gather_rows(plan, parts, tokens):
-    depth = parts[0].shape[1]
-    hbm = pl.BlockSpec(memory_space=pltpu.HBM)
-    return pl.pallas_call(
-        functools.partial(gather_kernel, plan),
-        in_specs=vmem(len(parts)),
-        out_specs=[hbm, hbm],
-        out_shape=[pltpu.HBM((tokens, depth), BF16)] * 2,
-        scratch_shapes=[pltpu.VMEM((tokens, depth), BF16), pltpu.SemaphoreType.DMA((4,))],
-        compiler_params=limit(6),
-        name="gather_rows",
-    )(*(near(part) for part in parts))
-
-
-def last_kernel(plan, *refs):
-    parts, refs = refs[:2], refs[2:]
-    grad, loss, _, _, next_act, next_grad, mean_loss, wide, sems = refs
+            wide[...] = jnp.zeros_like(wide)
+            copy(wide, next_act)
+
+    put_rows(plan, (one, two), (next_act, next_grad), row, sems, more)
+
+
+def loss_rows_kernel(plan, part, grad, loss, _a, _g, next_act, next_grad, mean_loss, wide, row, sems):
     last = len(plan) - 1
     mean_loss[...] = jnp.where(lax.axis_index("section") == last, loss[...], 0.0)
 
@@ -518,21 +595,11 @@
             wide[...] = jnp.broadcast_to(grad[...], wide.shape).astype(BF16)
             copy(wide, next_grad)
 
-    put_rows(plan, parts, (next_act, next_grad), sems, more)
-
-
-def last_rows(plan, parts, grad, loss, next_act, next_grad):
-    hbm = pl.BlockSpec(memory_space=pltpu.HBM)
-    return pl.pallas_call(
-        functools.partial(last_kernel, plan),
-        in_specs=vmem(4) + [hbm, hbm],
-        out_specs=[hbm, hbm] + vmem(1),
-        out_shape=[pltpu.HBM(next_act.shape, BF16)] * 2 + [jax.ShapeDtypeStruct((1, lane), F32)],
-        input_output_aliases={4: 0, 5: 1},
-        scratch_shapes=[pltpu.VMEM(next_act.shape, BF16), pltpu.SemaphoreType.DMA((4,))],
-        compiler_params=limit(6),
-        name="last_rows",
-    )(near(parts[0]), near(parts[1]), near(grad), loss, next_act, next_grad)
+    put_rows(plan, (part,), (next_act, next_grad), row, sems, more)
+
+
+def last_kernel(plan, part, _a, _g, next_act, next_grad, _wide, row, sems):
+    put_rows(plan, (part,), (next_act, next_grad), row, sems, lambda *_: None)
 
 
 def swap(value, axis, bit):
@@ -555,19 +622,18 @@
     _, _, tokens, depth = activations.shape
     rows = head_weight.shape[0]
     act, kept, cot = (value.reshape(tokens, depth) for value in (activations, saved, cotangents))
-    low = lane
-    high = tokens - low
     weight = projection[0]
 
     pack = pack_head(text_embed, head_weight)
     other = swap(pack, "section", 1)
-    send_one, hand = early_block(low, act, kept, cot, section_gain, weight)
+    send_one, hand = early_block(act, kept, cot, section_gain, weight)
     one = swap(send_one, "section", 1)
     hand_high = swap(hand, "section", 2)
     pooled, send_three, send_two = later_block(act, kept, cot, section_gain, weight, hand)
     two = swap(send_two, "section", 1)
     pair = swap(stack(pack, other), "section", 2)
     packs = (pack, other, pair)
+    text = own_text(packs, rows, depth)
 
     gain = final_gain.reshape(1, depth)
     table, standard = features(pooled, gain, labels)
@@ -578,7 +644,7 @@
         bit *= 2
     hand_low = swap(one, "section", 2)
     three = swap(choose(hand_high, send_three), "section", 1)
-    mine, send = embed(table, packs, rows)
+    mine, send = embed(table, text, packs, rows)
     bit = devices // 2
     while bit > 1:
         other = swap(send, "dp", bit)
@@ -587,21 +653,18 @@
     other = swap(send, "dp", 1)
     grad, loss = loss_step(mine, other, table, standard, gain, tokens)
     plan = (
-        ((1, high, 1, low),),
-        ((0, low, 0, 0), (1, high, 0, low)),
-        ((0, low, 1, 0), (1, high, 1, low)),
-        ((1, high, 0, low),),
-    )
-    next_act, next_grad = gather_rows(plan, (one, two), tokens)
-    plan = (
-        ((0, low, 1, 0),),
-        ((1, low, 1, 0), (0, high, 1, low)),
-        ((1, low, 0, 0), (0, high, 0, low)),
-        ((0, low, 0, 0),),
-    )
-    next_act, next_grad, mean_loss = last_rows(
-        plan, (three, hand_low), grad, loss, next_act, next_grad
-    )
+        ((1, 1, lane, True),),
+        ((0, 0, 0, False), (1, 0, lane, True)),
+        ((0, 1, 0, False), (1, 1, lane, True)),
+        ((1, 0, lane, True),),
+    )
+    outs = rows_call(gather_kernel, plan, (one, two), (), tokens, depth)
+    plan = ((), ((0, 1, 0, False),), ((0, 0, 0, False),), ())
+    *outs, mean_loss = rows_call(
+        loss_rows_kernel, plan, (hand_low,), (grad, loss), tokens, depth, outs
+    )
+    plan = (((0, 1, 0, False),), ((0, 1, lane, True),), ((0, 0, lane, True),), ((0, 0, 0, False),))
+    next_act, next_grad = rows_call(last_kernel, plan, (three,), (), tokens, depth, outs)
     return (next_act[None, None], next_grad[None, None], mean_loss[0, 0:1])
 
 
@@ -735,14 +798,14 @@
     return (next_act, next_grad, mean_loss)
 
 
-def fits(mesh, width):
+def fits(mesh, width, tokens):
     sections, devices = mesh.shape["section"], mesh.shape["dp"]
     power = devices > 1 and not (devices & (devices - 1))
-    return sections == 4 and power and width == devices * lane
+    return sections == 4 and power and width == devices * lane and 0 < tokens - 2 * lane <= 8
 
 
 def either(mesh, *args):
-    if fits(mesh, args[7].shape[1]):
+    if fits(mesh, args[7].shape[1], args[0].shape[2]):
         return local(*args)
     return plain_local(*args)
 

time: 60.8 us -> 62.3 us (1.025)
  Pallas kernels: 8.22 us -> 9.24 us
    pallas_call x2 -> x4, Pallas kernels: 2.47 us -> 3.28 us  [the longest x3 3.26 us: rows_call(): pl.pallas_call(functools.partial(kernel, plan), in_specs=vmem(count) + [h...]
  transfers between devices with their start and end apart: 13 -> 13, of which waited for: 6 -> 5; matrix products, arithmetic and copies ran while one was open for 0% -> 0% of each run, Pallas kernels for 7% -> 8%
where the time goes in v3:
time: 62.3 us; the launch traced here: 61.5 us
  starting transfers between devices  22 us (35%)
  waiting for transfers between devices  20.8 us (33%)
  Pallas kernels  9.24 us (15%)
  local copies, waits for them, and re-layouts  7.78 us (12%)
  between operations  1.57 us (3%)
    ppermute x13, starting transfers between devices, swap(): lax.ppermute(value, axis, [(index, index ^ bit) for index in range(count)])  22 us
    ppermute x13, waiting for transfers between devices, swap(): lax.ppermute(value, axis, [(index, index ^ bit) for index in range(count)])  20.8 us
    unnamed x10, local copies, waits for them, and re-layouts  7.08 us
    pallas_call x3, Pallas kernels, rows_call(): pl.pallas_call(functools.partial(kernel, plan), in_specs=vmem(count) + [h...  3.26 us
    pallas_call x1, Pallas kernels, early_block(): pl.pallas_call(early_kernel, in_specs=vmem(5), out_specs=vmem(2), out_sha...  2.46 us
    pallas_call x1, Pallas kernels, pack_head(): pl.pallas_call(pack_kernel, in_specs=[pl.BlockSpec(memory_space=pl.ANY)]...  1.73 us
  transfers between devices with their start and end apart: 13, of which 5 were waited for; matrix products, arithmetic and copies ran while one was open for 0% of the time, Pallas kernels for 8%

profile of v3, /device:TPU:0, one launch (start us, length us, event | category | flops | bytes accessed | tf_op | source)
XLA Modules:
  0.0 61.5 jit_solution(18328357479570489846)
XLA Ops:
  1.3 0.7 %reshape.21.gain = f32[1,1792]{1,0:T(1,128)S(1)} reshape(f32[1792]{0:T(1024)} %param.14) | data formatting | bytes 14336 | tf_op jit(solution)/shard_map/reshape | solution.py:638
  2.0 2.8 %copy-done = bf16[1,1792,1792]{2,1,0:T(8,128)(2,1)S(1)} copy-done((bf16[1,1792,1792]{2,1,0:T(8,128)(2,1)S(1)}, bf16[1,1792,1792]{2,1,0:T(8,128)(2,1)}, u32[]{:S(2)}) %copy-start) | copy-done | bytes 6422552
  4.8 1.2 %copy-done.1 = bf16[1,1,257,1792]{3,2,1,0:T(8,128)(2,1)S(1)} copy-done((bf16[1,1,257,1792]{3,2,1,0:T(8,128)(2,1)S(1)}, bf16[1,1,257,1792]{3,2,1,0:T(8,128)(2,1)}, u32[]{:S(2)}) %copy-start.1) | copy-done | bytes 921112
  6.0 1.2 %copy-done.2 = bf16[1,1,257,1792]{3,2,1,0:T(8,128)(2,1)S(1)} copy-done((bf16[1,1,257,1792]{3,2,1,0:T(8,128)(2,1)S(1)}, bf16[1,1,257,1792]{3,2,1,0:T(8,128)(2,1)}, u32[]{:S(2)}) %copy-start.2) | copy-done | bytes 921112
  7.2 1.2 %copy-done.3 = bf16[1,1,257,1792]{3,2,1,0:T(8,128)(2,1)S(1)} copy-done((bf16[1,1,257,1792]{3,2,1,0:T(8,128)(2,1)S(1)}, bf16[1,1,257,1792]{3,2,1,0:T(8,128)(2,1)}, u32[]{:S(2)}) %copy-start.3) | copy-done | bytes 921112
  8.4 0.7 %copy-done.4 = f32[1,1792]{1,0:T(1,128)S(1)} copy-done((f32[1,1792]{1,0:T(1,128)S(1)}, f32[1,1792]{1,0:T(1,128)}, u32[]{:S(2)}) %copy-start.4) | copy-done | bytes 7192
  9.1 2.5 %early_block.1 = (bf16[128,1792]{1,0:T(8,128)(2,1)S(1)}, bf16[1808,128]{1,0:T(8,128)(2,1)S(1)}) custom-call(bf16[257,1792]{1,0:T(8,128)(2,1)S(1)} %bitcast.10, bf16[257,1792]{1,0:T(8,128)(2,1)S(1)} %bitcast.12, bf16[257,1792]{1,0:T(8,128)(2,1)S(1)} %bitcast.14, f32[1,1792]{1,0:T(1,128)S(1)} %copy-done.4, bf16[1792,1792]{1,0:T(8,128)(2,1)S(1)} %bitcast.8), custom_call_target="tpu_custom_call" | custom-call | flops 1650589696 | bytes 6422528 | tf_op jit(solution)/shard_map/early_block/pallas_call | solution.py:195
  11.5 0.3 later_block.1
  11.8 0.2 features.1
  12.1 0.6 collective-permute-start.4
  12.6 5.5 %collective-permute-start = (bf16[1808,128]{1,0:T(8,128)(2,1)S(1)}, bf16[1808,128]{1,0:T(8,128)(2,1)S(1)}, u32[]{:S(2)}, u32[]{:S(2)}) collective-permute-start(bf16[1808,128]{1,0:T(8,128)(2,1)S(1)} %get-tuple-element.25.hand), channel_id=1, source_target_pairs={{0,16},{8,24},{16,0},{24,8},{1,17},{9,25},{17,1},{25,9},{2,18},{10... | collective-permute-start | bytes 1388552 | tf_op jit(solution)/shard_map/ppermute | solution.py:607
  18.1 1.6 %collective-permute-start.2 = (bf16[128,1792]{1,0:T(8,128)(2,1)S(1)}, bf16[128,1792]{1,0:T(8,128)(2,1)S(1)}, u32[]{:S(2)}, u32[]{:S(2)}) collective-permute-start(bf16[128,1792]{1,0:T(8,128)(2,1)S(1)} %get-tuple-element.27), channel_id=1, source_target_pairs={{0,8},{8,0},{16,24},{24,16},{1,9},{9,1},{17,25},{25,17},{2,10},{10... | collective-permute-start | bytes 1376264 | tf_op jit(solution)/shard_map/ppermute | solution.py:607
  19.8 1.6 %collective-permute-start.5 = (f32[2,1920]{1,0:T(2,128)S(1)}, f32[2,1920]{1,0:T(2,128)S(1)}, u32[]{:S(2)}, u32[]{:S(2)}) collective-permute-start(f32[2,1920]{1,0:T(2,128)S(1)} %pad_maximum_fusion.2), channel_id=1, source_target_pairs={{0,2},{1,3},{2,0},{3,1},{4,6},{5,7},{6,4},{7,5},{8,10},{9,11},{10,... | collective-permute-start | bytes 46088 | tf_op jit(solution)/shard_map/ppermute | solution.py:607
  21.4 1.7 %pack_head.1.first.refs_0_ = bf16[464,128]{1,0:T(8,128)(2,1)S(1)} custom-call(bf16[1,1024]{1,0:T(2,128)(2,1)} %text_hbm.1, bf16[448,1024]{1,0:T(8,128)(2,1)} %head_hbm.1), custom_call_target="tpu_custom_call" | custom-call | flops 8000000000 | bytes 917504 | tf_op jit(solution)/shard_map/pack_head/pallas_call | solution.py:124
  23.1 0.5 collective-permute-start.7
  23.7 1.6 %collective-permute-start.12 = (bf16[1808,128]{1,0:T(8,128)(2,1)S(1)}, bf16[1808,128]{1,0:T(8,128)(2,1)S(1)}, u32[]{:S(2)}, u32[]{:S(2)}) collective-permute-start(bf16[1808,128]{1,0:T(8,128)(2,1)S(1)} %get-tuple-element.39), channel_id=1, source_target_pairs={{0,8},{8,0},{16,24},{24,16},{1,9},{9,1},{17,25},{25,17},{2,10},{10... | collective-permute-start | bytes 1388552 | tf_op jit(solution)/shard_map/ppermute | solution.py:607
  25.2 6.3 %collective-permute-done.2.one = bf16[128,1792]{1,0:T(8,128)(2,1)S(1)} collective-permute-done((bf16[128,1792]{1,0:T(8,128)(2,1)S(1)}, bf16[128,1792]{1,0:T(8,128)(2,1)S(1)}, u32[]{:S(2)}, u32[]{:S(2)}) %collective-permute-start.2) | collective-permute-done | bytes 458784 | tf_op jit(solution)/shard_map/ppermute | solution.py:607
  31.5 0.1 collective-permute-start.3
  31.7 2.0 %collective-permute-start.1 = (bf16[1808,128]{1,0:T(8,128)(2,1)S(1)}, bf16[1808,128]{1,0:T(8,128)(2,1)S(1)}, u32[]{:S(2)}, u32[]{:S(2)}) collective-permute-start(bf16[1808,128]{1,0:T(8,128)(2,1)S(1)} %choose.1), channel_id=1, source_target_pairs={{0,8},{8,0},{16,24},{24,16},{1,9},{9,1},{17,25},{25,17},{2,10},{10... | collective-permute-start | bytes 1388552 | tf_op jit(solution)/shard_map/ppermute | solution.py:607
  33.7 2.7 %collective-permute-start.6 = (f32[4,1920]{1,0:T(4,128)S(1)}, f32[4,1920]{1,0:T(4,128)S(1)}, u32[]{:S(2)}, u32[]{:S(2)}) collective-permute-start(f32[4,1920]{1,0:T(4,128)S(1)} %pad_maximum_fusion.1), channel_id=1, source_target_pairs={{0,4},{1,5},{2,6},{3,7},{4,0},{5,1},{6,2},{7,3},{8,12},{9,13},{10,... | collective-permute-start | bytes 92168 | tf_op jit(solution)/shard_map/ppermute | solution.py:607
  36.4 1.6 %collective-permute-start.8 = (bf16[928,128]{1,0:T(8,128)(2,1)S(1)}, bf16[928,128]{1,0:T(8,128)(2,1)S(1)}, u32[]{:S(2)}, u32[]{:S(2)}) collective-permute-start(bf16[928,128]{1,0:T(8,128)(2,1)S(1)} %stack.1), channel_id=1, source_target_pairs={{0,16},{8,24},{16,0},{24,8},{1,17},{9,25},{17,1},{25,9},{2,18},{10... | collective-permute-start | bytes 712712 | tf_op jit(solution)/shard_map/ppermute | solution.py:607
  38.0 0.5 collective-permute-done.6
  38.6 8.9 %collective-permute-done.8.refs_2_ = bf16[928,128]{1,0:T(8,128)(2,1)S(1)} collective-permute-done((bf16[928,128]{1,0:T(8,128)(2,1)S(1)}, bf16[928,128]{1,0:T(8,128)(2,1)S(1)}, u32[]{:S(2)}, u32[]{:S(2)}) %collective-permute-start.8) | collective-permute-done | bytes 237600 | tf_op jit(solution)/shard_map/ppermute | solution.py:607
  47.6 0.4 embed.1
  48.0 2.6 %collective-permute-start.9 = (f32[5,1920]{1,0:T(8,128)S(1)}, f32[5,1920]{1,0:T(8,128)S(1)}, u32[]{:S(2)}, u32[]{:S(2)}) collective-permute-start(f32[5,1920]{1,0:T(8,128)S(1)} %get-tuple-element.31), channel_id=1, source_target_pairs={{0,4},{1,5},{2,6},{3,7},{4,0},{5,1},{6,2},{7,3},{8,12},{9,13},{10,... | collective-permute-start | bytes 115208 | tf_op jit(solution)/shard_map/ppermute | solution.py:607
  50.6 2.6 %collective-permute-done.9.theirs = f32[5,1920]{1,0:T(8,128)S(1)} collective-permute-done((f32[5,1920]{1,0:T(8,128)S(1)}, f32[5,1920]{1,0:T(8,128)S(1)}, u32[]{:S(2)}, u32[]{:S(2)}) %collective-permute-start.9) | collective-permute-done | bytes 38432 | tf_op jit(solution)/shard_map/ppermute | solution.py:607
  53.3 1.5 %collective-permute-start.10 = (f32[4,1920]{1,0:T(4,128)S(1)}, f32[4,1920]{1,0:T(4,128)S(1)}, u32[]{:S(2)}, u32[]{:S(2)}) collective-permute-start(f32[4,1920]{1,0:T(4,128)S(1)} %get-tuple-element.33), channel_id=1, source_target_pairs={{0,2},{1,3},{2,0},{3,1},{4,6},{5,7},{6,4},{7,5},{8,10},{9,11},{10,... | collective-permute-start | bytes 92168 | tf_op jit(solution)/shard_map/ppermute | solution.py:607
  54.8 2.4 %collective-permute-done.10.theirs = f32[4,1920]{1,0:T(4,128)S(1)} collective-permute-done((f32[4,1920]{1,0:T(4,128)S(1)}, f32[4,1920]{1,0:T(4,128)S(1)}, u32[]{:S(2)}, u32[]{:S(2)}) %collective-permute-start.10) | collective-permute-done | bytes 30752 | tf_op jit(solution)/shard_map/ppermute | solution.py:607
  57.4 1.4 %shard_map.112 = (bf16[257,1792]{1,0:T(8,128)(2,1)}, bf16[257,1792]{1,0:T(8,128)(2,1)}) custom-call(bf16[128,1792]{1,0:T(8,128)(2,1)S(1)} %collective-permute-done.2.one, bf16[1808,128]{1,0:T(8,128)(2,1)S(1)} %collective-permute-done.12.two), custom_call_target="tpu_custom_call" | custom-call | tf_op jit(solution)/shard_map/pallas_call | solution.py:565
  58.8 0.6 %loss_step.1 = (f32[1,1792]{1,0:T(1,128)S(1)}, f32[1,128]{1,0:T(1,128)S(1)}) custom-call(f32[5,1920]{1,0:T(8,128)S(1)} %get-tuple-element.34.mine, f32[5,1920]{1,0:T(8,128)S(1)} %collective-permute-done.11.theirs, f32[8,1920]{1,0:T(8,128)S(1)} %pad_maximum_fusion.table, f32[1,1920]{1,0:T(1,128)S(1)} %get-tuple-element.36.standard, f32[1,1792]{1,0:T(1,128)S(1)} %reshape.21.gain), custom_call_target="tpu_custom_call" | custom-call | tf_op jit(solution)/shard_map/loss_step/pallas_call | solution.py:461
  59.4 0.8 %shard_map.113 = (bf16[257,1792]{1,0:T(8,128)(2,1)}, bf16[257,1792]{1,0:T(8,128)(2,1)}, f32[1,128]{1,0:T(1,128)}) custom-call(bf16[128,1792]{1,0:T(8,128)(2,1)S(1)} %collective-permute-done.3.part, f32[1,1792]{1,0:T(1,128)S(1)} %get-tuple-element.37.grad, f32[1,128]{1,0:T(1,128)S(1)} %get-tuple-element.38.loss, ...), custom_call_target="tpu_custom_call", output_to_operand_aliasing={{0}: (3, {}), {1}: (4, {})} | custom-call | tf_op jit(solution)/shard_map/pallas_call | solution.py:565
  60.3 1.1 %shard_map.114 = (bf16[257,1792]{1,0:T(8,128)(2,1)}, bf16[257,1792]{1,0:T(8,128)(2,1)}) custom-call(bf16[1808,128]{1,0:T(8,128)(2,1)S(1)} %collective-permute-done.1.part, bf16[257,1792]{1,0:T(8,128)(2,1)} %get-tuple-element.42._a, bf16[257,1792]{1,0:T(8,128)(2,1)} %get-tuple-element.43._g), custom_call_target="tpu_custom_call", output_to_operand_aliasing={{0}: (1, {}), {1}: (2, {})} | custom-call | tf_op jit(solution)/shard_map/pallas_call | solution.py:565
  (22 shorter events, 0.3 us)
Async XLA Ops:
  2.0 2.8 %copy-start = (bf16[1,1792,1792]{2,1,0:T(8,128)(2,1)S(1)}, bf16[1,1792,1792]{2,1,0:T(8,128)(2,1)}, u32[]{:S(2)}) copy-start(bf16[1,1792,1792]{2,1,0:T(8,128)(2,1)} %param.12) | copy-start | bytes 19267588
  4.8 1.2 %copy-start.1 = (bf16[1,1,257,1792]{3,2,1,0:T(8,128)(2,1)S(1)}, bf16[1,1,257,1792]{3,2,1,0:T(8,128)(2,1)}, u32[]{:S(2)}) copy-start(bf16[1,1,257,1792]{3,2,1,0:T(8,128)(2,1)} %param.9) | copy-start | bytes 2763268
  6.0 1.2 %copy-start.2 = (bf16[1,1,257,1792]{3,2,1,0:T(8,128)(2,1)S(1)}, bf16[1,1,257,1792]{3,2,1,0:T(8,128)(2,1)}, u32[]{:S(2)}) copy-start(bf16[1,1,257,1792]{3,2,1,0:T(8,128)(2,1)} %param.10) | copy-start | bytes 2763268
  7.2 1.2 %copy-start.3 = (bf16[1,1,257,1792]{3,2,1,0:T(8,128)(2,1)S(1)}, bf16[1,1,257,1792]{3,2,1,0:T(8,128)(2,1)}, u32[]{:S(2)}) copy-start(bf16[1,1,257,1792]{3,2,1,0:T(8,128)(2,1)} %param.11) | copy-start | bytes 2763268
  8.4 0.7 %copy-start.4 = (f32[1,1792]{1,0:T(1,128)S(1)}, f32[1,1792]{1,0:T(1,128)}, u32[]{:S(2)}) copy-start(f32[1,1792]{1,0:T(1,128)} %gain.3) | copy-start | bytes 21508
  12.1 7.7 %collective-permute-start.4 = (f32[1,1920]{1,0:T(1,128)S(1)}, f32[1,1920]{1,0:T(1,128)S(1)}, u32[]{:S(2)}, u32[]{:S(2)}) collective-permute-start(f32[1,1920]{1,0:T(1,128)S(1)} %get-tuple-element.29), channel_id=1, source_target_pairs={{0,1},{1,0},{2,3},{3,2},{4,5},{5,4},{6,7},{7,6},{8,9},{9,8},{10,11... | collective-permute-start | bytes 23048 | tf_op jit(solution)/shard_map/ppermute | solution.py:607
  12.6 19.0 %collective-permute-start = (bf16[1808,128]{1,0:T(8,128)(2,1)S(1)}, bf16[1808,128]{1,0:T(8,128)(2,1)S(1)}, u32[]{:S(2)}, u32[]{:S(2)}) collective-permute-start(bf16[1808,128]{1,0:T(8,128)(2,1)S(1)} %get-tuple-element.25.hand), channel_id=1, source_target_pairs={{0,16},{8,24},{16,0},{24,8},{1,17},{9,25},{17,1},{25,9},{2,18},{10... | collective-permute-start | bytes 1388552 | tf_op jit(solution)/shard_map/ppermute | solution.py:607
  18.1 13.4 %collective-permute-start.2 = (bf16[128,1792]{1,0:T(8,128)(2,1)S(1)}, bf16[128,1792]{1,0:T(8,128)(2,1)S(1)}, u32[]{:S(2)}, u32[]{:S(2)}) collective-permute-start(bf16[128,1792]{1,0:T(8,128)(2,1)S(1)} %get-tuple-element.27), channel_id=1, source_target_pairs={{0,8},{8,0},{16,24},{24,16},{1,9},{9,1},{17,25},{25,17},{2,10},{10... | collective-permute-start | bytes 1376264 | tf_op jit(solution)/shard_map/ppermute | solution.py:607
  19.8 13.9 %collective-permute-start.5 = (f32[2,1920]{1,0:T(2,128)S(1)}, f32[2,1920]{1,0:T(2,128)S(1)}, u32[]{:S(2)}, u32[]{:S(2)}) collective-permute-start(f32[2,1920]{1,0:T(2,128)S(1)} %pad_maximum_fusion.2), channel_id=1, source_target_pairs={{0,2},{1,3},{2,0},{3,1},{4,6},{5,7},{6,4},{7,5},{8,10},{9,11},{10,... | collective-permute-start | bytes 46088 | tf_op jit(solution)/shard_map/ppermute | solution.py:607
  23.1 13.2 %collective-permute-start.7 = (bf16[464,128]{1,0:T(8,128)(2,1)S(1)}, bf16[464,128]{1,0:T(8,128)(2,1)S(1)}, u32[]{:S(2)}, u32[]{:S(2)}) collective-permute-start(bf16[464,128]{1,0:T(8,128)(2,1)S(1)} %pack_head.1.first.refs_0_), channel_id=1, source_target_pairs={{0,8},{8,0},{16,24},{24,16},{1,9},{9,1},{17,25},{25,17},{2,10},{10... | collective-permute-start | bytes 356360 | tf_op jit(solution)/shard_map/ppermute | solution.py:607
  23.7 33.7 %collective-permute-start.12 = (bf16[1808,128]{1,0:T(8,128)(2,1)S(1)}, bf16[1808,128]{1,0:T(8,128)(2,1)S(1)}, u32[]{:S(2)}, u32[]{:S(2)}) collective-permute-start(bf16[1808,128]{1,0:T(8,128)(2,1)S(1)} %get-tuple-element.39), channel_id=1, source_target_pairs={{0,8},{8,0},{16,24},{24,16},{1,9},{9,1},{17,25},{25,17},{2,10},{10... | collective-permute-start | bytes 1388552 | tf_op jit(solution)/shard_map/ppermute | solution.py:607
  31.5 27.9 %collective-permute-start.3 = (bf16[128,1792]{1,0:T(8,128)(2,1)S(1)}, bf16[128,1792]{1,0:T(8,128)(2,1)S(1)}, u32[]{:S(2)}, u32[]{:S(2)}) collective-permute-start(bf16[128,1792]{1,0:T(8,128)(2,1)S(1)} %collective-permute-done.2.one), channel_id=1, source_target_pairs={{0,16},{8,24},{16,0},{24,8},{1,17},{9,25},{17,1},{25,9},{2,18},{10... | collective-permute-start | bytes 1376264 | tf_op jit(solution)/shard_map/ppermute | solution.py:607
  31.7 28.6 %collective-permute-start.1 = (bf16[1808,128]{1,0:T(8,128)(2,1)S(1)}, bf16[1808,128]{1,0:T(8,128)(2,1)S(1)}, u32[]{:S(2)}, u32[]{:S(2)}) collective-permute-start(bf16[1808,128]{1,0:T(8,128)(2,1)S(1)} %choose.1), channel_id=1, source_target_pairs={{0,8},{8,0},{16,24},{24,16},{1,9},{9,1},{17,25},{25,17},{2,10},{10... | collective-permute-start | bytes 1388552 | tf_op jit(solution)/shard_map/ppermute | solution.py:607
  33.7 4.9 %collective-permute-start.6 = (f32[4,1920]{1,0:T(4,128)S(1)}, f32[4,1920]{1,0:T(4,128)S(1)}, u32[]{:S(2)}, u32[]{:S(2)}) collective-permute-start(f32[4,1920]{1,0:T(4,128)S(1)} %pad_maximum_fusion.1), channel_id=1, source_target_pairs={{0,4},{1,5},{2,6},{3,7},{4,0},{5,1},{6,2},{7,3},{8,12},{9,13},{10,... | collective-permute-start | bytes 92168 | tf_op jit(solution)/shard_map/ppermute | solution.py:607
  36.4 11.1 %collective-permute-start.8 = (bf16[928,128]{1,0:T(8,128)(2,1)S(1)}, bf16[928,128]{1,0:T(8,128)(2,1)S(1)}, u32[]{:S(2)}, u32[]{:S(2)}) collective-permute-start(bf16[928,128]{1,0:T(8,128)(2,1)S(1)} %stack.1), channel_id=1, source_target_pairs={{0,16},{8,24},{16,0},{24,8},{1,17},{9,25},{17,1},{25,9},{2,18},{10... | collective-permute-start | bytes 712712 | tf_op jit(solution)/shard_map/ppermute | solution.py:607
  48.0 5.3 %collective-permute-start.9 = (f32[5,1920]{1,0:T(8,128)S(1)}, f32[5,1920]{1,0:T(8,128)S(1)}, u32[]{:S(2)}, u32[]{:S(2)}) collective-permute-start(f32[5,1920]{1,0:T(8,128)S(1)} %get-tuple-element.31), channel_id=1, source_target_pairs={{0,4},{1,5},{2,6},{3,7},{4,0},{5,1},{6,2},{7,3},{8,12},{9,13},{10,... | collective-permute-start | bytes 115208 | tf_op jit(solution)/shard_map/ppermute | solution.py:607
  53.3 3.9 %collective-permute-start.10 = (f32[4,1920]{1,0:T(4,128)S(1)}, f32[4,1920]{1,0:T(4,128)S(1)}, u32[]{:S(2)}, u32[]{:S(2)}) collective-permute-start(f32[4,1920]{1,0:T(4,128)S(1)} %get-tuple-element.33), channel_id=1, source_target_pairs={{0,2},{1,3},{2,0},{3,1},{4,6},{5,7},{6,4},{7,5},{8,10},{9,11},{10,... | collective-permute-start | bytes 92168 | tf_op jit(solution)/shard_map/ppermute | solution.py:607
  57.3 1.4 %collective-permute-start.11 = (f32[5,1920]{1,0:T(8,128)S(1)}, f32[5,1920]{1,0:T(8,128)S(1)}, u32[]{:S(2)}, u32[]{:S(2)}) collective-permute-start(f32[5,1920]{1,0:T(8,128)S(1)} %get-tuple-element.35), channel_id=1, source_target_pairs={{0,1},{1,0},{2,3},{3,2},{4,5},{5,4},{6,7},{7,6},{8,9},{9,8},{10,11... | collective-permute-start | bytes 115208 | tf_op jit(solution)/shard_map/ppermute | solution.py:607

commit v4 on v3

--- a/solution.py
+++ b/solution.py
@@ -74,13 +74,13 @@
         grad = dot(cot[...], weight[low:high], NT) * gain[:, low:high]
         grads[:, low:high] = grad
         total = total + jnp.sum(grad, axis=-1, keepdims=True)
-        unit = (saved[:, low:high].astype(F32) - centre) * inverse
-        total_unit = total_unit + jnp.sum(grad * unit, axis=-1, keepdims=True)
-    mean = total * (1.0 / depth)
-    mean_unit = total_unit * (1.0 / depth)
+        centred = saved[:, low:high].astype(F32) - centre
+        total_unit = total_unit + jnp.sum(grad * centred, axis=-1, keepdims=True)
+    mean = inverse * total * (1.0 / depth)
+    slope = inverse * (inverse * (inverse * total_unit * (1.0 / depth)))
     for low, high in tiles_of(depth):
-        unit = (saved[:, low:high].astype(F32) - centre) * inverse
-        block = inverse * (grads[:, low:high] - mean - unit * mean_unit)
+        centred = saved[:, low:high].astype(F32) - centre
+        block = (inverse * grads[:, low:high] - mean) - centred * slope
         put(low, high, (cot[:, low:high].astype(F32) + block).astype(BF16))
 
 

time: 62.3 us -> 62.3 us (level)
  no operation moved by 1% of the time
where the time goes in v4:
time: 62.3 us; the launch traced here: 61.5 us
  starting transfers between devices  22 us (35%)
  waiting for transfers between devices  20.8 us (33%)
  Pallas kernels  9.24 us (15%)
  local copies, waits for them, and re-layouts  7.78 us (12%)
  between operations  1.57 us (3%)
    ppermute x13, starting transfers between devices, swap(): lax.ppermute(value, axis, [(index, index ^ bit) for index in range(count)])  22 us
    ppermute x13, waiting for transfers between devices, swap(): lax.ppermute(value, axis, [(index, index ^ bit) for index in range(count)])  20.8 us
    unnamed x10, local copies, waits for them, and re-layouts  7.08 us
    pallas_call x3, Pallas kernels, rows_call(): pl.pallas_call(functools.partial(kernel, plan), in_specs=vmem(count) + [h...  3.26 us
    pallas_call x1, Pallas kernels, early_block(): pl.pallas_call(early_kernel, in_specs=vmem(5), out_specs=vmem(2), out_sha...  2.46 us
    pallas_call x1, Pallas kernels, pack_head(): pl.pallas_call(pack_kernel, in_specs=[pl.BlockSpec(memory_space=pl.ANY)]...  1.73 us
  transfers between devices with their start and end apart: 13, of which 5 were waited for; matrix products, arithmetic and copies ran while one was open for 0% of the time, Pallas kernels for 8%

profile of v4, /device:TPU:0, one launch (start us, length us, event | category | flops | bytes accessed | tf_op | source)
XLA Modules:
  0.0 61.5 jit_solution(7241420198996666293)
XLA Ops:
  1.3 0.7 %reshape.21.gain = f32[1,1792]{1,0:T(1,128)S(1)} reshape(f32[1792]{0:T(1024)} %param.14) | data formatting | bytes 14336 | tf_op jit(solution)/shard_map/reshape | solution.py:638
  2.0 2.8 %copy-done = bf16[1,1792,1792]{2,1,0:T(8,128)(2,1)S(1)} copy-done((bf16[1,1792,1792]{2,1,0:T(8,128)(2,1)S(1)}, bf16[1,1792,1792]{2,1,0:T(8,128)(2,1)}, u32[]{:S(2)}) %copy-start) | copy-done | bytes 6422552
  4.8 1.2 %copy-done.1 = bf16[1,1,257,1792]{3,2,1,0:T(8,128)(2,1)S(1)} copy-done((bf16[1,1,257,1792]{3,2,1,0:T(8,128)(2,1)S(1)}, bf16[1,1,257,1792]{3,2,1,0:T(8,128)(2,1)}, u32[]{:S(2)}) %copy-start.1) | copy-done | bytes 921112
  6.0 1.2 %copy-done.2 = bf16[1,1,257,1792]{3,2,1,0:T(8,128)(2,1)S(1)} copy-done((bf16[1,1,257,1792]{3,2,1,0:T(8,128)(2,1)S(1)}, bf16[1,1,257,1792]{3,2,1,0:T(8,128)(2,1)}, u32[]{:S(2)}) %copy-start.2) | copy-done | bytes 921112
  7.2 1.2 %copy-done.3 = bf16[1,1,257,1792]{3,2,1,0:T(8,128)(2,1)S(1)} copy-done((bf16[1,1,257,1792]{3,2,1,0:T(8,128)(2,1)S(1)}, bf16[1,1,257,1792]{3,2,1,0:T(8,128)(2,1)}, u32[]{:S(2)}) %copy-start.3) | copy-done | bytes 921112
  8.4 0.7 %copy-done.4 = f32[1,1792]{1,0:T(1,128)S(1)} copy-done((f32[1,1792]{1,0:T(1,128)S(1)}, f32[1,1792]{1,0:T(1,128)}, u32[]{:S(2)}) %copy-start.4) | copy-done | bytes 7192
  9.1 2.5 %early_block.1 = (bf16[128,1792]{1,0:T(8,128)(2,1)S(1)}, bf16[1808,128]{1,0:T(8,128)(2,1)S(1)}) custom-call(bf16[257,1792]{1,0:T(8,128)(2,1)S(1)} %bitcast.10, bf16[257,1792]{1,0:T(8,128)(2,1)S(1)} %bitcast.12, bf16[257,1792]{1,0:T(8,128)(2,1)S(1)} %bitcast.14, f32[1,1792]{1,0:T(1,128)S(1)} %copy-done.4, bf16[1792,1792]{1,0:T(8,128)(2,1)S(1)} %bitcast.8), custom_call_target="tpu_custom_call" | custom-call | flops 1650589696 | bytes 6422528 | tf_op jit(solution)/shard_map/early_block/pallas_call | solution.py:195
  11.5 0.3 later_block.1
  11.8 0.2 features.1
  12.1 0.6 collective-permute-start.4
  12.6 5.6 %collective-permute-start = (bf16[1808,128]{1,0:T(8,128)(2,1)S(1)}, bf16[1808,128]{1,0:T(8,128)(2,1)S(1)}, u32[]{:S(2)}, u32[]{:S(2)}) collective-permute-start(bf16[1808,128]{1,0:T(8,128)(2,1)S(1)} %get-tuple-element.25.hand), channel_id=1, source_target_pairs={{0,16},{8,24},{16,0},{24,8},{1,17},{9,25},{17,1},{25,9},{2,18},{10... | collective-permute-start | bytes 1388552 | tf_op jit(solution)/shard_map/ppermute | solution.py:607
  18.2 1.6 %collective-permute-start.2 = (bf16[128,1792]{1,0:T(8,128)(2,1)S(1)}, bf16[128,1792]{1,0:T(8,128)(2,1)S(1)}, u32[]{:S(2)}, u32[]{:S(2)}) collective-permute-start(bf16[128,1792]{1,0:T(8,128)(2,1)S(1)} %get-tuple-element.27), channel_id=1, source_target_pairs={{0,8},{8,0},{16,24},{24,16},{1,9},{9,1},{17,25},{25,17},{2,10},{10... | collective-permute-start | bytes 1376264 | tf_op jit(solution)/shard_map/ppermute | solution.py:607
  19.8 1.6 %collective-permute-start.5 = (f32[2,1920]{1,0:T(2,128)S(1)}, f32[2,1920]{1,0:T(2,128)S(1)}, u32[]{:S(2)}, u32[]{:S(2)}) collective-permute-start(f32[2,1920]{1,0:T(2,128)S(1)} %pad_maximum_fusion.2), channel_id=1, source_target_pairs={{0,2},{1,3},{2,0},{3,1},{4,6},{5,7},{6,4},{7,5},{8,10},{9,11},{10,... | collective-permute-start | bytes 46088 | tf_op jit(solution)/shard_map/ppermute | solution.py:607
  21.4 1.7 %pack_head.1.first.refs_0_ = bf16[464,128]{1,0:T(8,128)(2,1)S(1)} custom-call(bf16[1,1024]{1,0:T(2,128)(2,1)} %text_hbm.1, bf16[448,1024]{1,0:T(8,128)(2,1)} %head_hbm.1), custom_call_target="tpu_custom_call" | custom-call | flops 8000000000 | bytes 917504 | tf_op jit(solution)/shard_map/pack_head/pallas_call | solution.py:124
  23.2 0.5 collective-permute-start.7
  23.7 1.6 %collective-permute-start.12 = (bf16[1808,128]{1,0:T(8,128)(2,1)S(1)}, bf16[1808,128]{1,0:T(8,128)(2,1)S(1)}, u32[]{:S(2)}, u32[]{:S(2)}) collective-permute-start(bf16[1808,128]{1,0:T(8,128)(2,1)S(1)} %get-tuple-element.39), channel_id=1, source_target_pairs={{0,8},{8,0},{16,24},{24,16},{1,9},{9,1},{17,25},{25,17},{2,10},{10... | collective-permute-start | bytes 1388552 | tf_op jit(solution)/shard_map/ppermute | solution.py:607
  25.3 6.3 %collective-permute-done.2.one = bf16[128,1792]{1,0:T(8,128)(2,1)S(1)} collective-permute-done((bf16[128,1792]{1,0:T(8,128)(2,1)S(1)}, bf16[128,1792]{1,0:T(8,128)(2,1)S(1)}, u32[]{:S(2)}, u32[]{:S(2)}) %collective-permute-start.2) | collective-permute-done | bytes 458784 | tf_op jit(solution)/shard_map/ppermute | solution.py:607
  31.6 0.1 collective-permute-start.3
  31.7 2.0 %collective-permute-start.1 = (bf16[1808,128]{1,0:T(8,128)(2,1)S(1)}, bf16[1808,128]{1,0:T(8,128)(2,1)S(1)}, u32[]{:S(2)}, u32[]{:S(2)}) collective-permute-start(bf16[1808,128]{1,0:T(8,128)(2,1)S(1)} %choose.1), channel_id=1, source_target_pairs={{0,8},{8,0},{16,24},{24,16},{1,9},{9,1},{17,25},{25,17},{2,10},{10... | collective-permute-start | bytes 1388552 | tf_op jit(solution)/shard_map/ppermute | solution.py:607
  33.7 2.7 %collective-permute-start.6 = (f32[4,1920]{1,0:T(4,128)S(1)}, f32[4,1920]{1,0:T(4,128)S(1)}, u32[]{:S(2)}, u32[]{:S(2)}) collective-permute-start(f32[4,1920]{1,0:T(4,128)S(1)} %pad_maximum_fusion.1), channel_id=1, source_target_pairs={{0,4},{1,5},{2,6},{3,7},{4,0},{5,1},{6,2},{7,3},{8,12},{9,13},{10,... | collective-permute-start | bytes 92168 | tf_op jit(solution)/shard_map/ppermute | solution.py:607
  36.4 1.7 %collective-permute-start.8 = (bf16[928,128]{1,0:T(8,128)(2,1)S(1)}, bf16[928,128]{1,0:T(8,128)(2,1)S(1)}, u32[]{:S(2)}, u32[]{:S(2)}) collective-permute-start(bf16[928,128]{1,0:T(8,128)(2,1)S(1)} %stack.1), channel_id=1, source_target_pairs={{0,16},{8,24},{16,0},{24,8},{1,17},{9,25},{17,1},{25,9},{2,18},{10... | collective-permute-start | bytes 712712 | tf_op jit(solution)/shard_map/ppermute | solution.py:607
  38.1 0.5 collective-permute-done.6
  38.6 8.9 %collective-permute-done.8.refs_2_ = bf16[928,128]{1,0:T(8,128)(2,1)S(1)} collective-permute-done((bf16[928,128]{1,0:T(8,128)(2,1)S(1)}, bf16[928,128]{1,0:T(8,128)(2,1)S(1)}, u32[]{:S(2)}, u32[]{:S(2)}) %collective-permute-start.8) | collective-permute-done | bytes 237600 | tf_op jit(solution)/shard_map/ppermute | solution.py:607
  47.6 0.4 embed.1
  48.0 2.6 %collective-permute-start.9 = (f32[5,1920]{1,0:T(8,128)S(1)}, f32[5,1920]{1,0:T(8,128)S(1)}, u32[]{:S(2)}, u32[]{:S(2)}) collective-permute-start(f32[5,1920]{1,0:T(8,128)S(1)} %get-tuple-element.31), channel_id=1, source_target_pairs={{0,4},{1,5},{2,6},{3,7},{4,0},{5,1},{6,2},{7,3},{8,12},{9,13},{10,... | collective-permute-start | bytes 115208 | tf_op jit(solution)/shard_map/ppermute | solution.py:607
  50.7 2.6 %collective-permute-done.9.theirs = f32[5,1920]{1,0:T(8,128)S(1)} collective-permute-done((f32[5,1920]{1,0:T(8,128)S(1)}, f32[5,1920]{1,0:T(8,128)S(1)}, u32[]{:S(2)}, u32[]{:S(2)}) %collective-permute-start.9) | collective-permute-done | bytes 38432 | tf_op jit(solution)/shard_map/ppermute | solution.py:607
  53.4 1.5 %collective-permute-start.10 = (f32[4,1920]{1,0:T(4,128)S(1)}, f32[4,1920]{1,0:T(4,128)S(1)}, u32[]{:S(2)}, u32[]{:S(2)}) collective-permute-start(f32[4,1920]{1,0:T(4,128)S(1)} %get-tuple-element.33), channel_id=1, source_target_pairs={{0,2},{1,3},{2,0},{3,1},{4,6},{5,7},{6,4},{7,5},{8,10},{9,11},{10,... | collective-permute-start | bytes 92168 | tf_op jit(solution)/shard_map/ppermute | solution.py:607
  54.9 2.4 %collective-permute-done.10.theirs = f32[4,1920]{1,0:T(4,128)S(1)} collective-permute-done((f32[4,1920]{1,0:T(4,128)S(1)}, f32[4,1920]{1,0:T(4,128)S(1)}, u32[]{:S(2)}, u32[]{:S(2)}) %collective-permute-start.10) | collective-permute-done | bytes 30752 | tf_op jit(solution)/shard_map/ppermute | solution.py:607
  57.4 1.4 %shard_map.112 = (bf16[257,1792]{1,0:T(8,128)(2,1)}, bf16[257,1792]{1,0:T(8,128)(2,1)}) custom-call(bf16[128,1792]{1,0:T(8,128)(2,1)S(1)} %collective-permute-done.2.one, bf16[1808,128]{1,0:T(8,128)(2,1)S(1)} %collective-permute-done.12.two), custom_call_target="tpu_custom_call" | custom-call | tf_op jit(solution)/shard_map/pallas_call | solution.py:565
  58.8 0.6 %loss_step.1 = (f32[1,1792]{1,0:T(1,128)S(1)}, f32[1,128]{1,0:T(1,128)S(1)}) custom-call(f32[5,1920]{1,0:T(8,128)S(1)} %get-tuple-element.34.mine, f32[5,1920]{1,0:T(8,128)S(1)} %collective-permute-done.11.theirs, f32[8,1920]{1,0:T(8,128)S(1)} %pad_maximum_fusion.table, f32[1,1920]{1,0:T(1,128)S(1)} %get-tuple-element.36.standard, f32[1,1792]{1,0:T(1,128)S(1)} %reshape.21.gain), custom_call_target="tpu_custom_call" | custom-call | tf_op jit(solution)/shard_map/loss_step/pallas_call | solution.py:461
  59.5 0.8 %shard_map.113 = (bf16[257,1792]{1,0:T(8,128)(2,1)}, bf16[257,1792]{1,0:T(8,128)(2,1)}, f32[1,128]{1,0:T(1,128)}) custom-call(bf16[128,1792]{1,0:T(8,128)(2,1)S(1)} %collective-permute-done.3.part, f32[1,1792]{1,0:T(1,128)S(1)} %get-tuple-element.37.grad, f32[1,128]{1,0:T(1,128)S(1)} %get-tuple-element.38.loss, ...), custom_call_target="tpu_custom_call", output_to_operand_aliasing={{0}: (3, {}), {1}: (4, {})} | custom-call | tf_op jit(solution)/shard_map/pallas_call | solution.py:565
  60.3 1.1 %shard_map.114 = (bf16[257,1792]{1,0:T(8,128)(2,1)}, bf16[257,1792]{1,0:T(8,128)(2,1)}) custom-call(bf16[1808,128]{1,0:T(8,128)(2,1)S(1)} %collective-permute-done.1.part, bf16[257,1792]{1,0:T(8,128)(2,1)} %get-tuple-element.42._a, bf16[257,1792]{1,0:T(8,128)(2,1)} %get-tuple-element.43._g), custom_call_target="tpu_custom_call", output_to_operand_aliasing={{0}: (1, {}), {1}: (2, {})} | custom-call | tf_op jit(solution)/shard_map/pallas_call | solution.py:565
  (22 shorter events, 0.3 us)
Async XLA Ops:
  2.0 2.8 %copy-start = (bf16[1,1792,1792]{2,1,0:T(8,128)(2,1)S(1)}, bf16[1,1792,1792]{2,1,0:T(8,128)(2,1)}, u32[]{:S(2)}) copy-start(bf16[1,1792,1792]{2,1,0:T(8,128)(2,1)} %param.12) | copy-start | bytes 19267588
  4.8 1.2 %copy-start.1 = (bf16[1,1,257,1792]{3,2,1,0:T(8,128)(2,1)S(1)}, bf16[1,1,257,1792]{3,2,1,0:T(8,128)(2,1)}, u32[]{:S(2)}) copy-start(bf16[1,1,257,1792]{3,2,1,0:T(8,128)(2,1)} %param.9) | copy-start | bytes 2763268
  6.0 1.2 %copy-start.2 = (bf16[1,1,257,1792]{3,2,1,0:T(8,128)(2,1)S(1)}, bf16[1,1,257,1792]{3,2,1,0:T(8,128)(2,1)}, u32[]{:S(2)}) copy-start(bf16[1,1,257,1792]{3,2,1,0:T(8,128)(2,1)} %param.10) | copy-start | bytes 2763268
  7.2 1.2 %copy-start.3 = (bf16[1,1,257,1792]{3,2,1,0:T(8,128)(2,1)S(1)}, bf16[1,1,257,1792]{3,2,1,0:T(8,128)(2,1)}, u32[]{:S(2)}) copy-start(bf16[1,1,257,1792]{3,2,1,0:T(8,128)(2,1)} %param.11) | copy-start | bytes 2763268
  8.4 0.7 %copy-start.4 = (f32[1,1792]{1,0:T(1,128)S(1)}, f32[1,1792]{1,0:T(1,128)}, u32[]{:S(2)}) copy-start(f32[1,1792]{1,0:T(1,128)} %gain.3) | copy-start | bytes 21508
  12.1 7.7 %collective-permute-start.4 = (f32[1,1920]{1,0:T(1,128)S(1)}, f32[1,1920]{1,0:T(1,128)S(1)}, u32[]{:S(2)}, u32[]{:S(2)}) collective-permute-start(f32[1,1920]{1,0:T(1,128)S(1)} %get-tuple-element.29), channel_id=1, source_target_pairs={{0,1},{1,0},{2,3},{3,2},{4,5},{5,4},{6,7},{7,6},{8,9},{9,8},{10,11... | collective-permute-start | bytes 23048 | tf_op jit(solution)/shard_map/ppermute | solution.py:607
  12.6 19.0 %collective-permute-start = (bf16[1808,128]{1,0:T(8,128)(2,1)S(1)}, bf16[1808,128]{1,0:T(8,128)(2,1)S(1)}, u32[]{:S(2)}, u32[]{:S(2)}) collective-permute-start(bf16[1808,128]{1,0:T(8,128)(2,1)S(1)} %get-tuple-element.25.hand), channel_id=1, source_target_pairs={{0,16},{8,24},{16,0},{24,8},{1,17},{9,25},{17,1},{25,9},{2,18},{10... | collective-permute-start | bytes 1388552 | tf_op jit(solution)/shard_map/ppermute | solution.py:607
  18.2 13.4 %collective-permute-start.2 = (bf16[128,1792]{1,0:T(8,128)(2,1)S(1)}, bf16[128,1792]{1,0:T(8,128)(2,1)S(1)}, u32[]{:S(2)}, u32[]{:S(2)}) collective-permute-start(bf16[128,1792]{1,0:T(8,128)(2,1)S(1)} %get-tuple-element.27), channel_id=1, source_target_pairs={{0,8},{8,0},{16,24},{24,16},{1,9},{9,1},{17,25},{25,17},{2,10},{10... | collective-permute-start | bytes 1376264 | tf_op jit(solution)/shard_map/ppermute | solution.py:607
  19.8 13.9 %collective-permute-start.5 = (f32[2,1920]{1,0:T(2,128)S(1)}, f32[2,1920]{1,0:T(2,128)S(1)}, u32[]{:S(2)}, u32[]{:S(2)}) collective-permute-start(f32[2,1920]{1,0:T(2,128)S(1)} %pad_maximum_fusion.2), channel_id=1, source_target_pairs={{0,2},{1,3},{2,0},{3,1},{4,6},{5,7},{6,4},{7,5},{8,10},{9,11},{10,... | collective-permute-start | bytes 46088 | tf_op jit(solution)/shard_map/ppermute | solution.py:607
  23.2 13.2 %collective-permute-start.7 = (bf16[464,128]{1,0:T(8,128)(2,1)S(1)}, bf16[464,128]{1,0:T(8,128)(2,1)S(1)}, u32[]{:S(2)}, u32[]{:S(2)}) collective-permute-start(bf16[464,128]{1,0:T(8,128)(2,1)S(1)} %pack_head.1.first.refs_0_), channel_id=1, source_target_pairs={{0,8},{8,0},{16,24},{24,16},{1,9},{9,1},{17,25},{25,17},{2,10},{10... | collective-permute-start | bytes 356360 | tf_op jit(solution)/shard_map/ppermute | solution.py:607
  23.7 33.7 %collective-permute-start.12 = (bf16[1808,128]{1,0:T(8,128)(2,1)S(1)}, bf16[1808,128]{1,0:T(8,128)(2,1)S(1)}, u32[]{:S(2)}, u32[]{:S(2)}) collective-permute-start(bf16[1808,128]{1,0:T(8,128)(2,1)S(1)} %get-tuple-element.39), channel_id=1, source_target_pairs={{0,8},{8,0},{16,24},{24,16},{1,9},{9,1},{17,25},{25,17},{2,10},{10... | collective-permute-start | bytes 1388552 | tf_op jit(solution)/shard_map/ppermute | solution.py:607
  31.6 27.9 %collective-permute-start.3 = (bf16[128,1792]{1,0:T(8,128)(2,1)S(1)}, bf16[128,1792]{1,0:T(8,128)(2,1)S(1)}, u32[]{:S(2)}, u32[]{:S(2)}) collective-permute-start(bf16[128,1792]{1,0:T(8,128)(2,1)S(1)} %collective-permute-done.2.one), channel_id=1, source_target_pairs={{0,16},{8,24},{16,0},{24,8},{1,17},{9,25},{17,1},{25,9},{2,18},{10... | collective-permute-start | bytes 1376264 | tf_op jit(solution)/shard_map/ppermute | solution.py:607
  31.7 28.6 %collective-permute-start.1 = (bf16[1808,128]{1,0:T(8,128)(2,1)S(1)}, bf16[1808,128]{1,0:T(8,128)(2,1)S(1)}, u32[]{:S(2)}, u32[]{:S(2)}) collective-permute-start(bf16[1808,128]{1,0:T(8,128)(2,1)S(1)} %choose.1), channel_id=1, source_target_pairs={{0,8},{8,0},{16,24},{24,16},{1,9},{9,1},{17,25},{25,17},{2,10},{10... | collective-permute-start | bytes 1388552 | tf_op jit(solution)/shard_map/ppermute | solution.py:607
  33.7 4.9 %collective-permute-start.6 = (f32[4,1920]{1,0:T(4,128)S(1)}, f32[4,1920]{1,0:T(4,128)S(1)}, u32[]{:S(2)}, u32[]{:S(2)}) collective-permute-start(f32[4,1920]{1,0:T(4,128)S(1)} %pad_maximum_fusion.1), channel_id=1, source_target_pairs={{0,4},{1,5},{2,6},{3,7},{4,0},{5,1},{6,2},{7,3},{8,12},{9,13},{10,... | collective-permute-start | bytes 92168 | tf_op jit(solution)/shard_map/ppermute | solution.py:607
  36.4 11.2 %collective-permute-start.8 = (bf16[928,128]{1,0:T(8,128)(2,1)S(1)}, bf16[928,128]{1,0:T(8,128)(2,1)S(1)}, u32[]{:S(2)}, u32[]{:S(2)}) collective-permute-start(bf16[928,128]{1,0:T(8,128)(2,1)S(1)} %stack.1), channel_id=1, source_target_pairs={{0,16},{8,24},{16,0},{24,8},{1,17},{9,25},{17,1},{25,9},{2,18},{10... | collective-permute-start | bytes 712712 | tf_op jit(solution)/shard_map/ppermute | solution.py:607
  48.0 5.3 %collective-permute-start.9 = (f32[5,1920]{1,0:T(8,128)S(1)}, f32[5,1920]{1,0:T(8,128)S(1)}, u32[]{:S(2)}, u32[]{:S(2)}) collective-permute-start(f32[5,1920]{1,0:T(8,128)S(1)} %get-tuple-element.31), channel_id=1, source_target_pairs={{0,4},{1,5},{2,6},{3,7},{4,0},{5,1},{6,2},{7,3},{8,12},{9,13},{10,... | collective-permute-start | bytes 115208 | tf_op jit(solution)/shard_map/ppermute | solution.py:607
  53.4 3.9 %collective-permute-start.10 = (f32[4,1920]{1,0:T(4,128)S(1)}, f32[4,1920]{1,0:T(4,128)S(1)}, u32[]{:S(2)}, u32[]{:S(2)}) collective-permute-start(f32[4,1920]{1,0:T(4,128)S(1)} %get-tuple-element.33), channel_id=1, source_target_pairs={{0,2},{1,3},{2,0},{3,1},{4,6},{5,7},{6,4},{7,5},{8,10},{9,11},{10,... | collective-permute-start | bytes 92168 | tf_op jit(solution)/shard_map/ppermute | solution.py:607
  57.4 1.4 %collective-permute-start.11 = (f32[5,1920]{1,0:T(8,128)S(1)}, f32[5,1920]{1,0:T(8,128)S(1)}, u32[]{:S(2)}, u32[]{:S(2)}) collective-permute-start(f32[5,1920]{1,0:T(8,128)S(1)} %get-tuple-element.35), channel_id=1, source_target_pairs={{0,1},{1,0},{2,3},{3,2},{4,5},{5,4},{6,7},{7,6},{8,9},{9,8},{10,11... | collective-permute-start | bytes 115208 | tf_op jit(solution)/shard_map/ppermute | solution.py:607
